TPU v7x, 16 devices: a 4x2x1 block of a 4x4x8 slice. The times are simulated.
16 devices in a mesh: rep: 4 (over y, z, core), dp: 4 (over x).
Axes of the slice: x: 4, y: 2, z: 1, core: 2. Of those that a mesh axis runs over, the one named last changes fastest.
The devices are a block of a 4x4x8 slice.
Arguments:
- g_w_gate: bfloat16 [16, 2, 896, 2560], P(('rep', 'dp')), parts along dimension 0
- g_w_up: bfloat16 [16, 2, 896, 2560], P(('rep', 'dp')), parts along dimension 0
- g_w_down: bfloat16 [16, 2, 2560, 896], P(('rep', 'dp')), parts along dimension 0
- w_gate: bfloat16 [2, 896, 2560], replicated
- w_up: bfloat16 [2, 896, 2560], replicated
- w_down: bfloat16 [2, 2560, 896], replicated
- m_w_gate: float32 [2, 896, 2560], P(None, 'dp')
- m_w_up: float32 [2, 896, 2560], P(None, 'dp')
- m_w_down: float32 [2, 2560, 896], P(None, 'dp')
- v_w_gate: float32 [2, 896, 2560], P(None, 'dp')
- v_w_up: float32 [2, 896, 2560], P(None, 'dp')
- v_w_down: float32 [2, 2560, 896], P(None, 'dp')
Outputs:
- output 1: bfloat16 [8, 896, 2560], P('rep'), parts along dimension 0
- output 2: bfloat16 [8, 896, 2560], P('rep'), parts along dimension 0
- output 3: bfloat16 [8, 2560, 896], P('rep'), parts along dimension 0
- output 4: float32 [8, 896, 2560], P('rep', 'dp'), parts along dimension 0
- output 5: float32 [8, 896, 2560], P('rep', 'dp'), parts along dimension 0
- output 6: float32 [8, 2560, 896], P('rep', 'dp'), parts along dimension 0
- output 7: float32 [8, 896, 2560], P('rep', 'dp'), parts along dimension 0
- output 8: float32 [8, 896, 2560], P('rep', 'dp'), parts along dimension 0
- output 9: float32 [8, 2560, 896], P('rep', 'dp'), parts along dimension 0
There are 4 independent parts. A program takes and returns all parts, laid end to end along the dimension named above; an argument that names none is the same for every part.
All inputs are finite; a program needn't handle non-finite values.
Results may differ from a plain program's by a relative error of at most 0.022.
Values are sent between devices in bfloat16 or wider.
A program may use at most 768 MiB of HBM per device.

v0:
```python
import jax
import jax.numpy as jnp
from jax import lax
from jax.sharding import PartitionSpec as P


def adamw(w, m, v, g):
    m = 0.9 * m + 0.1 * g
    v = 0.95 * v + 0.05 * g * g
    step = m * lax.rsqrt(v + 1e-8) + 0.1 * w
    return (w - 0.02 * step).astype(jnp.bfloat16), m, v


def solution(mesh):
    def step(*arrays):
        terms, weights, m, v = (arrays[i : i + 3] for i in (0, 3, 6, 9))
        gradients = [lax.psum_scatter(t[0], "dp", scatter_dimension=1, tiled=True).astype(jnp.float32) for t in terms]
        me = lax.axis_index("dp")
        own = [lax.dynamic_slice_in_dim(w, me * one.shape[1], one.shape[1], 1).astype(jnp.float32) for w, one in zip(weights, m, strict=True)]
        new = [adamw(w, m, v, g) for w, m, v, g in zip(own, m, v, gradients, strict=True)]
        whole = [lax.all_gather(one[0], "dp", axis=1, tiled=True) for one in new]
        return (*whole, *(one[1] for one in new), *(one[2] for one in new))

    all_of, cut = P(None, None, None), P(None, "dp", None)
    return jax.shard_map(
        step,
        mesh=mesh,
        in_specs=(P(("rep", "dp"), None, None, None),) * 3 + (all_of,) * 3 + (cut,) * 6,
        out_specs=(P("rep", None, None),) * 3 + (P("rep", "dp", None),) * 6,
        check_vma=False,
    )
```

profile of v0, /device:TPU:112, one launch (start us, length us, event | category | flops | bytes accessed | tf_op | source)
XLA Modules:
  0.0 561.9 jit_solution(10008678176332030820)
XLA Ops:
  7.2 0.1 reduce-scatter.8.cloned.1.call-start
  7.3 0.7 reduce-scatter.8.cloned.1.call-update
  8.0 0.1 reduce-scatter.6.cloned.1.call-start
  8.1 0.7 reduce-scatter.6.cloned.1.call-update
  8.8 0.1 reduce-scatter.4.cloned.1.call-start
  8.9 0.7 reduce-scatter.4.cloned.1.call-update
  9.6 0.1 all-gather.8.cloned.1.call-start
  9.7 86.5 %reduce-scatter.8.cloned.1.call-done = bf16[2,640,896]{2,1,0:T(8,128)(2,1)} async-done(((bf16[2,2560,896]{2,1,0:T(8,128)(2,1)}), bf16[2,640,896]{2,1,0:T(8,128)(2,1)}) %reduce-scatter.8.cloned.1.call-update) | async-done | bytes 2293776 | tf_op jit(solution)/shard_map/reduce_scatter | solution.py:17
  96.1 9.3 %fusion.10 = (bf16[2,640,896]{2,1,0:T(8,128)(2,1)}, f32[2,640,896]{2,1,0:T(8,128)}, f32[2,640,896]{2,1,0:T(8,128)}) fusion(bf16[2,2560,896]{2,1,0:T(8,128)(2,1)} %param.17, s32[]{:T(128)S(6)} %select_n.8, bf16[2,640,896]{2,1,0:T(8,128)(2,1)} %reduce-scatter.8.cloned.1.call-done, f32[2,640,896]{2,1,0:T(8,128)} %param.23, f32[2,640,896]{2,1,0:T(8,128)} %param.20), kind=kLoop, calls=%fused_computation.22 | loop fusion | flops 18350080 | bytes 25231364 | tf_op jit(solution)/shard_map/convert_element_type | solution.py:11
  105.5 0.1 all-gather.8.cloned.1.call-update
  105.5 0.1 all-gather.6.cloned.1.call-start
  105.6 75.5 %reduce-scatter.6.cloned.1.call-done = bf16[2,224,2560]{2,1,0:T(8,128)(2,1)} async-done(((bf16[2,896,2560]{2,1,0:T(8,128)(2,1)}), bf16[2,224,2560]{2,1,0:T(8,128)(2,1)}) %reduce-scatter.6.cloned.1.call-update) | async-done | bytes 2293776 | tf_op jit(solution)/shard_map/reduce_scatter | solution.py:17
  181.0 9.2 %fusion.6 = (bf16[2,224,2560]{2,1,0:T(8,128)(2,1)}, f32[2,224,2560]{2,1,0:T(8,128)}, f32[2,224,2560]{2,1,0:T(8,128)}) fusion(bf16[2,896,2560]{2,1,0:T(8,128)(2,1)} %param.16, s32[]{:T(128)S(6)} %select_n.7, bf16[2,224,2560]{2,1,0:T(8,128)(2,1)} %reduce-scatter.6.cloned.1.call-done, f32[2,224,2560]{2,1,0:T(8,128)} %param.22, f32[2,224,2560]{2,1,0:T(8,128)} %param.19), kind=kLoop, calls=%fused_computation.18 | loop fusion | flops 18350080 | bytes 25231364 | tf_op jit(solution)/shard_map/convert_element_type | solution.py:11
  190.3 0.1 all-gather.6.cloned.1.call-update
  190.3 0.1 all-gather.4.cloned.1.call-start
  190.4 75.6 %reduce-scatter.4.cloned.1.call-done = bf16[2,224,2560]{2,1,0:T(8,128)(2,1)} async-done(((bf16[2,896,2560]{2,1,0:T(8,128)(2,1)}), bf16[2,224,2560]{2,1,0:T(8,128)(2,1)}) %reduce-scatter.4.cloned.1.call-update) | async-done | bytes 2293776 | tf_op jit(solution)/shard_map/reduce_scatter | solution.py:17
  266.0 9.2 %fusion.2 = (bf16[2,224,2560]{2,1,0:T(8,128)(2,1)}, f32[2,224,2560]{2,1,0:T(8,128)}, f32[2,224,2560]{2,1,0:T(8,128)}) fusion(bf16[2,896,2560]{2,1,0:T(8,128)(2,1)} %param.15, s32[]{:T(128)S(6)} %select_n.7, bf16[2,224,2560]{2,1,0:T(8,128)(2,1)} %reduce-scatter.4.cloned.1.call-done, f32[2,224,2560]{2,1,0:T(8,128)} %param.21, f32[2,224,2560]{2,1,0:T(8,128)} %param.18), kind=kLoop, calls=%fused_computation.14 | loop fusion | flops 18350080 | bytes 25231364 | tf_op jit(solution)/shard_map/convert_element_type | solution.py:11
  275.2 0.1 all-gather.4.cloned.1.call-update
  275.3 78.4 %all-gather.8.cloned.1.call-done = bf16[2,2560,896]{2,1,0:T(8,128)(2,1)} async-done(((bf16[2,640,896]{2,1,0:T(8,128)(2,1)}), bf16[2,2560,896]{2,1,0:T(8,128)(2,1)}) %all-gather.8.cloned.1.call-update) | async-done | bytes 9175056 | tf_op jit(solution)/shard_map/all_gather | solution.py:21
  353.6 88.9 %all-gather.6.cloned.1.call-done = bf16[2,896,2560]{2,1,0:T(8,128)(2,1)} async-done(((bf16[2,224,2560]{2,1,0:T(8,128)(2,1)}), bf16[2,896,2560]{2,1,0:T(8,128)(2,1)}) %all-gather.6.cloned.1.call-update) | async-done | bytes 9175056 | tf_op jit(solution)/shard_map/all_gather | solution.py:21
  442.5 88.9 %all-gather.4.cloned.1.call-done = bf16[2,896,2560]{2,1,0:T(8,128)(2,1)} async-done(((bf16[2,224,2560]{2,1,0:T(8,128)(2,1)}), bf16[2,896,2560]{2,1,0:T(8,128)(2,1)}) %all-gather.4.cloned.1.call-update) | async-done | bytes 9175056 | tf_op jit(solution)/shard_map/all_gather | solution.py:21
  531.4 7.8 %copy.24 = bf16[2,896,2560]{2,1,0:T(8,128)(2,1)} copy(bf16[2,896,2560]{2,1,0:T(8,128)(2,1)} %all-gather.4.cloned.1.call-done) | data formatting | bytes 18350080
  539.2 7.8 %copy.25 = bf16[2,896,2560]{2,1,0:T(8,128)(2,1)} copy(bf16[2,896,2560]{2,1,0:T(8,128)(2,1)} %all-gather.6.cloned.1.call-done) | data formatting | bytes 18350080
  547.1 8.0 %copy.26 = bf16[2,2560,896]{2,1,0:T(8,128)(2,1)} copy(bf16[2,2560,896]{2,1,0:T(8,128)(2,1)} %all-gather.8.cloned.1.call-done) | data formatting | bytes 18350080
Async XLA Ops:
  7.2 88.9 %reduce-scatter.8.cloned.1.call-start = ((), (), s32[]{:S(2)}) async-start(), calls=%async_computation.7 | async-start | bytes 11468800 | tf_op jit(solution)/shard_map/reduce_scatter | solution.py:17
  8.0 173.1 %reduce-scatter.6.cloned.1.call-start = ((), (), s32[]{:S(2)}) async-start(), calls=%async_computation.5 | async-start | bytes 11468800 | tf_op jit(solution)/shard_map/reduce_scatter | solution.py:17
  8.8 257.2 %reduce-scatter.4.cloned.1.call-start = ((), (), s32[]{:S(2)}) async-start(), calls=%async_computation.3 | async-start | bytes 11468800 | tf_op jit(solution)/shard_map/reduce_scatter | solution.py:17
  9.6 344.1 %all-gather.8.cloned.1.call-start = ((), (), s32[]{:S(2)}) async-start(), calls=%async_computation.8 | async-start | bytes 11468800 | tf_op jit(solution)/shard_map/all_gather | solution.py:21
  105.5 337.0 %all-gather.6.cloned.1.call-start = ((), (), s32[]{:S(2)}) async-start(), calls=%async_computation.6 | async-start | bytes 11468800 | tf_op jit(solution)/shard_map/all_gather | solution.py:21
  190.3 341.1 %all-gather.4.cloned.1.call-start = ((), (), s32[]{:S(2)}) async-start(), calls=%async_computation.4 | async-start | bytes 11468800 | tf_op jit(solution)/shard_map/all_gather | solution.py:21
Sparse Core Ops, SparseCore 0:
  10.4 85.6 reduce-scatter.7
  98.5 82.5 reduce-scatter.5
  183.4 82.5 reduce-scatter.3
  268.0 85.6 all-gather.7
  355.6 86.8 all-gather.5
  444.5 86.8 all-gather.3
where the time goes:
time: 562 us
  waiting for transfers between devices  496 us (88%)
  other arithmetic  27.8 us (5%)
  local copies, waits for them, and re-layouts  23.7 us (4%)
  between operations  14.2 us (3%)
    all_gather x3, waiting for transfers between devices, step(): whole = [lax.all_gather(one[0], 'dp', axis=1, tiled=True) for one in new]  256 us
    reduce_scatter x3, waiting for transfers between devices, step(): lax.psum_scatter(t[0], 'dp', scatter_dimension=1, tiled=True)  237 us
    convert_element_type x3, other arithmetic, adamw(): return ((w - 0.02 * step).astype(jnp.bfloat16), m, v)  27.8 us
    unnamed x3, local copies, waits for them, and re-layouts  23.7 us
  transfers between devices with their start and end apart: 6, of which 6 were waited for; matrix products, arithmetic and copies ran while one was open for 5% of the time, Pallas kernels for 0%

commit v1 on v0

v1 whole, which is shorter than its diff:
```python
import functools

import jax
import jax.numpy as jnp
from jax import lax
from jax.experimental import pallas as pl
from jax.experimental.pallas import tpu as pltpu
from jax.sharding import PartitionSpec as P

MESH = pl.DeviceIdType.MESH
BF16, F32 = jnp.bfloat16, jnp.float32
SENT = ("far_s", "far_r", "rel_s", "rel_r", "dir_s", "dir_r", "fwd_s", "fwd_r")
LOCAL = ("term", "own", "w", "m", "v", "g_out", "w_out")
BOTH_WAYS = ("near_s", "near_r")
SEMAPHORES = (*SENT, *LOCAL, *BOTH_WAYS)


def moments(m, v, g):
    return 0.9 * m + 0.1 * g, 0.95 * v + 0.05 * g * g


def weight(w, m, v):
    return w - 0.02 * (m * lax.rsqrt(v + 1e-8) + 0.1 * w)


def columns(width):
    parts = -(-width // 1024)
    while width % (parts * 128):
        parts += 1
    return [slice(i * (width // parts), (i + 1) * (width // parts)) for i in range(parts)]


def tiled(shape, body):
    def row(i, carry):
        rows = pl.ds(pl.multiple_of(i * 16, 16), 16)
        for cols in columns(shape[1]):
            body(rows, cols)
        return carry

    lax.fori_loop(0, shape[0] // 16, row, 0)


def kernel(n, layers, gathered, *refs):
    count = len(gathered)
    refs = list(refs)
    take = lambda k: [refs.pop(0) for _ in range(k)]
    g, w, m, v = take(count), take(count), take(count), take(count)
    g_out, w_out = take(count), take(count)
    far, rel, direct, term, own, new = (take(count) for _ in range(6))
    m_buf, v_buf = take(count), take(count)
    sem = dict(zip(SEMAPHORES, refs, strict=True))

    me = lax.axis_index("dp")
    right, left = lax.rem(me + 1, n), lax.rem(me + n - 1, n)
    opposite = lax.rem(me + 2, n)
    ahead, behind = (right, left), (left, right)

    barrier = pltpu.get_barrier_semaphore()
    for peer in (left, right):
        pl.semaphore_signal(barrier, inc=1, device_id={"dp": peer}, device_id_type=MESH)
    pl.semaphore_wait(barrier, 2)

    chunks = [(k, layer) for k in range(count) for layer in range(layers)]
    pending = []

    def rows(k, block, side):
        half = far[k].shape[2]
        return pl.ds(pl.multiple_of((2 * block + side) * half, 16), half)

    def send(src, dst, send_sem, recv_sem, peer):
        copy = pltpu.make_async_remote_copy(src, dst, send_sem, recv_sem, device_id={"dp": peer}, device_id_type=MESH)
        copy.start()
        pending.append(copy.wait_send)
        return copy

    def local(src, dst, s):
        copy = pltpu.make_async_copy(src, dst, s)
        copy.start()
        return copy

    sent, loads, steps = {}, {}, {}

    def first(c):
        k, l = chunks[c]
        for side in (0, 1):
            sent["far", c, side] = send(
                g[k].at[0, l, rows(k, opposite, side)], far[k].at[l, side], sem["far_s"].at[c, side], sem["far_r"].at[c, side], ahead[side]
            )
        for side in (0, 1):
            sent["dir", c, side] = send(
                g[k].at[0, l, rows(k, behind[side], side)], direct[k].at[l, side], sem["dir_s"].at[c, side], sem["dir_r"].at[c, side], behind[side]
            )
        for side in (0, 1):
            loads["term", c, side] = local(g[k].at[0, l, rows(k, ahead[side], side)], term[k].at[l, side], sem["term"].at[c, side])
        for side in (0, 1):
            loads["own", c, side] = local(g[k].at[0, l, rows(k, me, side)], own[k].at[l, side], sem["own"].at[c, side])
            loads["w", c, side] = local(w[k].at[l, rows(k, me, side)], new[k].at[l, side], sem["w"].at[c, side])

    def load_moments(c, side):
        k, l = chunks[c]
        half = far[k].shape[2]
        here = pl.ds(side * half, half)
        steps[c, side] = (
            local(m[k].at[l, here], m_buf[k].at[side], sem["m"].at[c, side]),
            local(v[k].at[l, here], v_buf[k].at[side], sem["v"].at[c, side]),
        )

    def relay(c):
        k, l = chunks[c]
        for side in (0, 1):
            sent["far", c, side].wait_recv()
            loads["term", c, side].wait()
            sums, mine = far[k].at[l, side], term[k].at[l, side]

            def add(r, cols):
                sums[r, cols] = (sums[r, cols].astype(F32) + mine[r, cols].astype(F32)).astype(BF16)

            tiled(sums.shape, add)
            sent["rel", c, side] = send(sums, rel[k].at[l, side], sem["rel_s"].at[c, side], sem["rel_r"].at[c, side], ahead[side])

    def step(c):
        k, l = chunks[c]
        half = far[k].shape[2]
        for side in (0, 1):
            sent["dir", c, side].wait_recv()
            sent["rel", c, side].wait_recv()
            loads["own", c, side].wait()
            loads["w", c, side].wait()
            for load in steps[c, side]:
                load.wait()
            a, b, o, x = (array[k].at[l, side] for array in (rel, direct, own, new))
            ms, vs = m_buf[k].at[side], v_buf[k].at[side]

            def update(r, cols):
                total = (a[r, cols].astype(F32) + b[r, cols].astype(F32) + o[r, cols].astype(F32)).astype(BF16)
                o[r, cols] = total
                m_new, v_new = moments(ms[r, cols], vs[r, cols], total.astype(F32))
                x[r, cols] = weight(x[r, cols].astype(F32), m_new, v_new).astype(BF16)

            tiled(o.shape, update)
            here = pl.ds(side * half, half)
            pending.append(local(o, g_out[k].at[l, here], sem["g_out"].at[c, side]).wait)
            if gathered[k]:
                place = w_out[k].at[l, rows(k, me, side)]
                for way, peer in enumerate((ahead[side], behind[side])):
                    sent["near", c, side, way] = send(x, place, sem["near_s"].at[c, side, way], sem["near_r"].at[c, side, way], peer)
            else:
                place = w_out[k].at[l, here]
            pending.append(local(x, place, sem["w_out"].at[c, side]).wait)
            if c + 1 < len(chunks):
                load_moments(c + 1, side)

    def forward(c):
        k, l = chunks[c]
        if not gathered[k]:
            return
        for side in (0, 1):
            sent["near", c, side, 0].wait_recv()
            place = w_out[k].at[l, rows(k, behind[side], side)]
            sent["fwd", c, side] = send(place, place, sem["fwd_s"].at[c, side], sem["fwd_r"].at[c, side], ahead[side])

    last = len(chunks)
    for c in range(min(2, last)):
        first(c)
    for side in (0, 1):
        load_moments(0, side)
    for c in range(last + 2):
        if c + 2 < last:
            first(c + 2)
        if c < last:
            relay(c)
        if 0 <= c - 1 < last:
            step(c - 1)
        if 0 <= c - 2 < last:
            forward(c - 2)
    for key, copy in sent.items():
        if key[0] == "fwd" or (key[0] == "near" and key[3] == 1):
            copy.wait_recv()
    for wait in pending:
        wait()


def reduce_and_step(n, gathered, terms, weights, m, v):
    layers = m[0].shape[0]
    count = len(terms)
    chunks = count * layers
    pieces = [(layers, 2, one.shape[1] // 2, one.shape[2]) for one in m]
    blocks = [jax.ShapeDtypeStruct(one.shape, BF16) for one in m]
    out_shape = blocks + [
        jax.ShapeDtypeStruct(w.shape if whole else one.shape, BF16) for w, one, whole in zip(weights, blocks, gathered, strict=True)
    ]
    sems = [pltpu.SemaphoreType.DMA((chunks, 2, 2) if name in BOTH_WAYS else (chunks, 2)) for name in SEMAPHORES]
    return pl.pallas_call(
        functools.partial(kernel, n, layers, gathered),
        out_shape=out_shape,
        in_specs=[pl.BlockSpec(memory_space=pl.ANY)] * (4 * count),
        out_specs=[pl.BlockSpec(memory_space=pl.ANY)] * (2 * count),
        scratch_shapes=[pltpu.VMEM(p, BF16) for _ in range(6) for p in pieces]
        + [pltpu.VMEM(p[1:], F32) for _ in range(2) for p in pieces]
        + sems,
        compiler_params=pltpu.CompilerParams(collective_id=0, has_side_effects=True, vmem_limit_bytes=66_000_000),
        name="reduce_and_step",
    )(*terms, *weights, *m, *v)


GATHERED = (True, True, True)


def solution(mesh):
    n = mesh.shape["dp"]

    def body(*arrays):
        terms, weights, m, v = (arrays[i : i + 3] for i in (0, 3, 6, 9))
        out = reduce_and_step(n, GATHERED, terms, weights, m, v)
        sums, new = out[:3], out[3:]
        pairs = [moments(m, v, g.astype(F32)) for m, v, g in zip(m, v, sums, strict=True)]
        return (*new, *(one[0] for one in pairs), *(one[1] for one in pairs))

    all_of, cut = P(None, None, None), P(None, "dp", None)
    return jax.shard_map(
        body,
        mesh=mesh,
        in_specs=(P(("rep", "dp"), None, None, None),) * 3 + (all_of,) * 3 + (cut,) * 6,
        out_specs=(P("rep", None, None),) * 3 + (P("rep", "dp", None),) * 6,
        check_vma=False,
    )
```

time: 562 us -> 496 us (0.88)
  waiting for transfers between devices: 496 us -> 0 us
  Pallas kernels: 0 us -> 450 us
  between operations: 14.2 us -> 0.69 us
  other arithmetic: 27.8 us -> 20.9 us
    pallas_call x0 -> x1, Pallas kernels: none -> 450 us  [reduce_and_step(): pl.pallas_call(functools.partial(kernel, n, layers, gathered), out_shape=...]
    all_gather x3 -> x0, waiting for transfers between devices: 256 us -> none  [step(): whole = [lax.all_gather(one[0], 'dp', axis=1, tiled=True) for one in new]]
    reduce_scatter x3 -> x0, waiting for transfers between devices: 237 us -> none  [step(): lax.psum_scatter(t[0], 'dp', scatter_dimension=1, tiled=True)]
    convert_element_type x3 -> x0, other arithmetic: 27.8 us -> none  [adamw(): return ((w - 0.02 * step).astype(jnp.bfloat16), m, v)]
    add x0 -> x2, other arithmetic: none -> 20.9 us  [moments(): return (0.9 * m + 0.1 * g, 0.95 * v + 0.05 * g * g)]
    unnamed x3 -> x9, local copies, waits for them, and re-layouts: 23.7 us -> 25 us
  transfers between devices with their start and end apart: 6 -> 0, of which waited for: 6 -> 0; matrix products, arithmetic and copies ran while one was open for 5% -> 0% of each run, Pallas kernels for 0% -> 0%
where the time goes in v1:
time: 496 us
  Pallas kernels  450 us (91%)
  local copies, waits for them, and re-layouts  25 us (5%)
  other arithmetic  20.9 us (4%)
    pallas_call x1, Pallas kernels, reduce_and_step(): pl.pallas_call(functools.partial(kernel, n, layers, gathered), out_shape=...  450 us
    unnamed x9, local copies, waits for them, and re-layouts  25 us
    add x2, other arithmetic, moments(): return (0.9 * m + 0.1 * g, 0.95 * v + 0.05 * g * g)  20.9 us

profile of v1, /device:TPU:112, one launch (start us, length us, event | category | flops | bytes accessed | tf_op | source)
XLA Modules:
  0.0 496.3 jit_solution(7755622875213719819)
XLA Ops:
  0.6 449.7 %reduce_and_step.1 = (bf16[2,224,2560]{2,1,0:T(8,128)(2,1)}, bf16[2,224,2560]{2,1,0:T(8,128)(2,1)}, bf16[2,640,896]{2,1,0:T(8,128)(2,1)}, bf16[2,896,2560]{2,1,0...) custom-call(bf16[1,2,896,2560]{3,2,1,0:T(8,128)(2,1)} %refs_0_.1, ...), custom_call_target="tpu_custom_call" | custom-call | tf_op jit(solution)/shard_map/reduce_and_step/pallas_call | solution.py:193
  450.4 0.0 copy-start
  450.4 0.0 copy-start.1
  450.4 0.0 copy-start.2
  450.4 16.0 %fusion.3 = (f32[2,224,2560]{2,1,0:T(8,128)}, f32[2,224,2560]{2,1,0:T(8,128)}, f32[2,224,2560]{2,1,0:T(8,128)}, f32[2,224,2560]{2,1,0:T(8,128)}) fusion(bf16[2,224,2560]{2,1,0:T(8,128)(2,1)} %get-tuple-element.18, f32[2,224,2560]{2,1,0:T(8,128)} %refs_9_.1, f32[2,224,2560]{2,1,0:T(8,128)} %refs_6_.1, bf16[2,224,2560]{2,1,0:T(8,128)(2,1)} %get-tuple-element.19, ...), kind=kLoop, calls=%fused_computation.9 | loop fusion | flops 18350080 | bytes 41287680 | tf_op jit(solution)/shard_map/add | solution.py:19
  466.4 0.0 copy-done
  466.4 0.0 copy-done.1
  466.4 1.3 copy-done.2
  467.7 4.9 fusion.5
  472.6 7.8 %copy.24 = bf16[2,896,2560]{2,1,0:T(8,128)(2,1)} copy(bf16[2,896,2560]{2,1,0:T(8,128)(2,1)} %get-tuple-element.38) | data formatting | bytes 18350080
  480.5 7.8 %copy.25 = bf16[2,896,2560]{2,1,0:T(8,128)(2,1)} copy(bf16[2,896,2560]{2,1,0:T(8,128)(2,1)} %get-tuple-element.39) | data formatting | bytes 18350080
  488.3 8.0 %copy.26 = bf16[2,2560,896]{2,1,0:T(8,128)(2,1)} copy(bf16[2,2560,896]{2,1,0:T(8,128)(2,1)} %get-tuple-element.40) | data formatting | bytes 18350080
Async XLA Ops:
  450.4 16.0 %copy-start = (f32[2,640,896]{2,1,0:T(8,128)S(1)}, f32[2,640,896]{2,1,0:T(8,128)}, u32[]{:S(2)}) copy-start(f32[2,640,896]{2,1,0:T(8,128)} %refs_8_.1) | copy-start | bytes 13762564
  450.4 16.0 %copy-start.1 = (f32[2,640,896]{2,1,0:T(8,128)S(1)}, f32[2,640,896]{2,1,0:T(8,128)}, u32[]{:S(2)}) copy-start(f32[2,640,896]{2,1,0:T(8,128)} %refs_11_.1) | copy-start | bytes 13762564
  450.4 17.3 %copy-start.2 = (bf16[2,640,896]{2,1,0:T(8,128)(2,1)S(1)}, bf16[2,640,896]{2,1,0:T(8,128)(2,1)}, u32[]{:S(2)}) copy-start(bf16[2,640,896]{2,1,0:T(8,128)(2,1)} %get-tuple-element.20) | copy-start | bytes 6881284

commit v2 on v1

--- a/solution.py
+++ b/solution.py
@@ -7,6 +7,7 @@
 from jax.experimental.pallas import tpu as pltpu
 from jax.sharding import PartitionSpec as P
 
+
 MESH = pl.DeviceIdType.MESH
 BF16, F32 = jnp.bfloat16, jnp.float32
 SENT = ("far_s", "far_r", "rel_s", "rel_r", "dir_s", "dir_r", "fwd_s", "fwd_r")
@@ -45,7 +46,8 @@
     refs = list(refs)
     take = lambda k: [refs.pop(0) for _ in range(k)]
     g, w, m, v = take(count), take(count), take(count), take(count)
-    g_out, w_out = take(count), take(count)
+    g_out = take(count)
+    w_out = [take(1)[0] if whole else [[refs.pop(0) for _ in range(2)] for _ in range(layers)] for whole in gathered]
     far, rel, direct, term, own, new = (take(count) for _ in range(6))
     m_buf, v_buf = take(count), take(count)
     sem = dict(zip(SEMAPHORES, refs, strict=True))
@@ -145,7 +147,7 @@
                 for way, peer in enumerate((ahead[side], behind[side])):
                     sent["near", c, side, way] = send(x, place, sem["near_s"].at[c, side, way], sem["near_r"].at[c, side, way], peer)
             else:
-                place = w_out[k].at[l, here]
+                place = w_out[k][l][side]
             pending.append(local(x, place, sem["w_out"].at[c, side]).wait)
             if c + 1 < len(chunks):
                 load_moments(c + 1, side)
@@ -186,15 +188,16 @@
     chunks = count * layers
     pieces = [(layers, 2, one.shape[1] // 2, one.shape[2]) for one in m]
     blocks = [jax.ShapeDtypeStruct(one.shape, BF16) for one in m]
-    out_shape = blocks + [
-        jax.ShapeDtypeStruct(w.shape if whole else one.shape, BF16) for w, one, whole in zip(weights, blocks, gathered, strict=True)
-    ]
+    new = []
+    for w, piece, whole in zip(weights, pieces, gathered, strict=True):
+        new += [jax.ShapeDtypeStruct(w.shape, BF16)] if whole else [jax.ShapeDtypeStruct(piece[2:], BF16)] * (2 * layers)
+    out_shape = blocks + new
     sems = [pltpu.SemaphoreType.DMA((chunks, 2, 2) if name in BOTH_WAYS else (chunks, 2)) for name in SEMAPHORES]
     return pl.pallas_call(
         functools.partial(kernel, n, layers, gathered),
         out_shape=out_shape,
         in_specs=[pl.BlockSpec(memory_space=pl.ANY)] * (4 * count),
-        out_specs=[pl.BlockSpec(memory_space=pl.ANY)] * (2 * count),
+        out_specs=[pl.BlockSpec(memory_space=pl.ANY)] * len(out_shape),
         scratch_shapes=[pltpu.VMEM(p, BF16) for _ in range(6) for p in pieces]
         + [pltpu.VMEM(p[1:], F32) for _ in range(2) for p in pieces]
         + sems,
@@ -203,22 +206,108 @@
     )(*terms, *weights, *m, *v)
 
 
-GATHERED = (True, True, True)
+def place_kernel(n, spots, *refs):
+    pieces = refs[: len(spots)]
+    out, buf, in_sem, out_sem = refs[len(spots) :]
+    me = lax.axis_index("dp")
+    half = buf.shape[1]
+    loads = []
+    for i, piece in enumerate(pieces):
+        copy = pltpu.make_async_copy(piece, buf.at[i], in_sem.at[i])
+        copy.start()
+        loads.append(copy)
+    stores = []
+    for i, (layer, side, offset) in enumerate(spots):
+        loads[i].wait()
+        row = pl.multiple_of((2 * lax.rem(me + offset, n) + side) * half, 16)
+        copy = pltpu.make_async_copy(buf.at[i], out.at[layer, pl.ds(row, half)], out_sem.at[i])
+        copy.start()
+        stores.append(copy)
+    for copy in stores:
+        copy.wait()
+
+
+def place(n, shape, pieces):
+    spots = tuple(pieces)
+    piece = pieces[spots[0]]
+    moved = 2 * len(spots) * piece.size * 2
+    return pl.pallas_call(
+        functools.partial(place_kernel, n, spots),
+        out_shape=jax.ShapeDtypeStruct(shape, BF16),
+        in_specs=[pl.BlockSpec(memory_space=pl.ANY)] * len(spots),
+        out_specs=pl.BlockSpec(memory_space=pl.ANY),
+        scratch_shapes=[pltpu.VMEM((len(spots), *piece.shape), BF16)] + [pltpu.SemaphoreType.DMA((len(spots),))] * 2,
+        cost_estimate=pl.CostEstimate(flops=moved, bytes_accessed=moved, transcendentals=0),
+        name="place",
+    )(*pieces.values())
+
+
+def finish_kernel(g, m, v, *refs):
+    m_out, v_out = refs[-2:]
+    m_out[...], v_out[...] = moments(m[...], v[...], g[...].astype(F32))
+    if len(refs) > 2:
+        w, w_out = refs[:2]
+        w_out[...] = w[...]
+
+
+def finish(g, m, v, *w):
+    layers, depth, width = m.shape
+    steps = next(k for k in range(7, 0, -1) if depth % (16 * k) == 0)
+    block = pl.BlockSpec((1, depth // steps, width), lambda l, i: (l, i, 0))
+    whole = [pl.BlockSpec((1, one.shape[1] // steps, width), lambda l, i: (l, i, 0)) for one in w]
+    moved = m.size * 18 + sum(one.size * 4 for one in w)
+    return pl.pallas_call(
+        finish_kernel,
+        grid=(layers, steps),
+        out_shape=[jax.ShapeDtypeStruct(one.shape, BF16) for one in w] + [jax.ShapeDtypeStruct(m.shape, F32)] * 2,
+        in_specs=[block] * 3 + whole,
+        out_specs=whole + [block] * 2,
+        cost_estimate=pl.CostEstimate(flops=moved, bytes_accessed=moved, transcendentals=0),
+    )(g, m, v, *w)
+
+
+def gather(n, shape, own):
+    right, left = ([(i, (i + way) % n) for i in range(n)] for way in (1, n - 1))
+    near, far = {}, {}
+    for layer, sides in enumerate(own):
+        for side, ahead in enumerate((right, left)):
+            near[layer, side, 0] = sides[side]
+            near[layer, side, (n - 1, 1)[side]] = lax.ppermute(sides[side], "dp", ahead)
+        for side, behind in enumerate((left, right)):
+            near[layer, side, (1, n - 1)[side]] = lax.ppermute(sides[side], "dp", behind)
+    for layer, sides in enumerate(own):
+        for side, ahead in enumerate((right, left)):
+            far[layer, side] = lax.ppermute(near[layer, side, (n - 1, 1)[side]], "dp", ahead)
+    whole = place(n, shape, near)
+    opposite = lax.rem(lax.axis_index("dp") + 2, n)
+    for (layer, side), piece in far.items():
+        whole = lax.dynamic_update_slice(whole, piece[None], (layer, (2 * opposite + side) * piece.shape[0], 0))
+    return whole
+
+
+GATHERED = (True, True, False)
 
 
 def solution(mesh):
     n = mesh.shape["dp"]
 
-    def body(*arrays):
+    def inner(*arrays):
         terms, weights, m, v = (arrays[i : i + 3] for i in (0, 3, 6, 9))
-        out = reduce_and_step(n, GATHERED, terms, weights, m, v)
-        sums, new = out[:3], out[3:]
-        pairs = [moments(m, v, g.astype(F32)) for m, v, g in zip(m, v, sums, strict=True)]
-        return (*new, *(one[0] for one in pairs), *(one[1] for one in pairs))
+        layers = m[0].shape[0]
+        out = list(reduce_and_step(n, GATHERED, terms, weights, m, v))
+        sums = [out.pop(0) for _ in range(3)]
+        new, m_new, v_new = [], [], []
+        for k, whole in enumerate(GATHERED):
+            held = [out.pop(0)] if whole else []
+            *w, a, b = finish(sums[k], m[k], v[k], *held)
+            new.append(w[0] if whole else gather(n, weights[k].shape, [[out.pop(0) for _ in range(2)] for _ in range(layers)]))
+            m_new.append(a)
+            v_new.append(b)
+        return (*new, *m_new, *v_new)
 
     all_of, cut = P(None, None, None), P(None, "dp", None)
     return jax.shard_map(
-        body,
+        inner,
         mesh=mesh,
         in_specs=(P(("rep", "dp"), None, None, None),) * 3 + (all_of,) * 3 + (cut,) * 6,
         out_specs=(P("rep", None, None),) * 3 + (P("rep", "dp", None),) * 6,

time: 496 us -> 483 us (0.974)
  waiting for transfers between devices: 0 us -> 31.5 us
  local copies, waits for them, and re-layouts: 25 us -> 3.44 us
  Pallas kernels: 450 us -> 429 us
  other arithmetic: 20.9 us -> 0 us
  starting transfers between devices: 0 us -> 17 us
    pallas_call x1, Pallas kernels: 450 us -> 376 us  [reduce_and_step(): pl.pallas_call(functools.partial(kernel, n, layers, gathered), out_shape=...]
    pallas_call x0 -> x4, Pallas kernels: none -> 52.4 us  [the longest x3 46.6 us: finish(): pl.pallas_call(finish_kernel, grid=(layers, steps), out_shape=[jax.ShapeD...]
    ppermute x0 -> x12, waiting for transfers between devices: none -> 31.5 us  [the longest x4 19.7 us: gather(): near[layer, side, (n - 1, 1)[side]] = lax.ppermute(sides[side], 'dp', ahead)]
    unnamed x9 -> x4, local copies, waits for them, and re-layouts: 25 us -> 0.01 us
    add x2 -> x0, other arithmetic: 20.9 us -> none  [moments(): return (0.9 * m + 0.1 * g, 0.95 * v + 0.05 * g * g)]
    ppermute x0 -> x12, starting transfers between devices: none -> 17 us  [the longest x4 7.02 us: gather(): lax.ppermute(near[layer, side, (n - 1, 1)[side]], 'dp', ahead)]
  transfers between devices with their start and end apart: 0 -> 12, of which waited for: 0 -> 3; matrix products, arithmetic and copies ran while one was open for 0% -> 1% of each run, Pallas kernels for 0% -> 11%
where the time goes in v2:
time: 483 us; the launch traced here: 481 us
  Pallas kernels  429 us (89%)
  waiting for transfers between devices  31.5 us (7%)
  starting transfers between devices  17 us (4%)
    pallas_call x1, Pallas kernels, reduce_and_step(): pl.pallas_call(functools.partial(kernel, n, layers, gathered), out_shape=...  376 us
    pallas_call x3, Pallas kernels, finish(): pl.pallas_call(finish_kernel, grid=(layers, steps), out_shape=[jax.ShapeD...  46.6 us
    ppermute x4, waiting for transfers between devices, gather(): near[layer, side, (n - 1, 1)[side]] = lax.ppermute(sides[side], 'dp', ahead)  19.7 us
    ppermute x4, waiting for transfers between devices, gather(): lax.ppermute(sides[side], 'dp', behind)  11.8 us
  transfers between devices with their start and end apart: 12, of which 3 were waited for; matrix products, arithmetic and copies ran while one was open for 1% of the time, Pallas kernels for 11%

profile of v2, /device:TPU:112, one launch (start us, length us, event | category | flops | bytes accessed | tf_op | source)
XLA Modules:
  0.0 481.3 jit_solution(16824128940825061244)
XLA Ops:
  0.6 376.3 %reduce_and_step.1 = (bf16[2,224,2560]{2,1,0:T(8,128)(2,1)}, bf16[2,224,2560]{2,1,0:T(8,128)(2,1)}, bf16[2,640,896]{2,1,0:T(8,128)(2,1)}, bf16[2,896,2560]{2,1,0...) custom-call(bf16[1,2,896,2560]{3,2,1,0:T(8,128)(2,1)} %refs_0_.1, ...), custom_call_target="tpu_custom_call" | custom-call | tf_op jit(solution)/shard_map/reduce_and_step/pallas_call | solution.py:196
  376.9 1.4 collective-permute-start
  378.3 1.9 collective-permute-start.1
  380.2 0.1 collective-permute-start.4
  380.4 3.1 collective-permute-start.5
  383.5 0.1 collective-permute-start.2
  383.6 10.8 %collective-permute-done.refs_1_ = bf16[320,896]{1,0:T(8,128)(2,1)} collective-permute-done((bf16[320,896]{1,0:T(8,128)(2,1)}, bf16[320,896]{1,0:T(8,128)(2,1)}, u32[]{:S(2)}, u32[]{:S(2)}) %collective-permute-start) | collective-permute-done | bytes 573472 | tf_op jit(solution)/shard_map/ppermute | solution.py:275
  394.4 0.1 collective-permute-start.3
  394.5 0.0 collective-permute-done.1.refs_3_
  394.5 3.1 collective-permute-start.6
  397.6 8.9 %collective-permute-done.4.refs_7_ = bf16[320,896]{1,0:T(8,128)(2,1)S(1)} collective-permute-done((bf16[320,896]{1,0:T(8,128)(2,1)}, bf16[320,896]{1,0:T(8,128)(2,1)S(1)}, u32[]{:S(2)}, u32[]{:S(2)}) %collective-permute-start.4) | collective-permute-done | bytes 573472 | tf_op jit(solution)/shard_map/ppermute | solution.py:275
  406.6 0.0 copy-start.1
  406.6 0.1 collective-permute-start.7
  406.7 0.0 collective-permute-done.5.refs_9_
  406.7 0.0 copy-start
  406.7 0.6 collective-permute-start.8
  407.3 11.8 %collective-permute-done.2.refs_4_ = bf16[320,896]{1,0:T(8,128)(2,1)} collective-permute-done((bf16[320,896]{1,0:T(8,128)(2,1)}, bf16[320,896]{1,0:T(8,128)(2,1)}, u32[]{:S(2)}, u32[]{:S(2)}) %collective-permute-start.2) | collective-permute-done | bytes 573472 | tf_op jit(solution)/shard_map/ppermute | solution.py:277
  419.1 3.1 collective-permute-start.9
  422.2 0.0 collective-permute-done.3.refs_5_
  422.2 0.0 collective-permute-start.10
  422.2 10.8 %shard_map.189 = (f32[2,640,896]{2,1,0:T(8,128)}, f32[2,640,896]{2,1,0:T(8,128)}) custom-call(bf16[2,640,896]{2,1,0:T(8,128)(2,1)} %get-tuple-element.38.g, f32[2,640,896]{2,1,0:T(8,128)} %m.5, f32[2,640,896]{2,1,0:T(8,128)} %v.5), custom_call_target="tpu_custom_call" | custom-call | flops 20643840 | bytes 20643840 | tf_op jit(solution)/shard_map/pallas_call | solution.py:259
  433.0 17.9 %shard_map.188 = (bf16[2,896,2560]{2,1,0:T(8,128)(2,1)}, f32[2,224,2560]{2,1,0:T(8,128)}, f32[2,224,2560]{2,1,0:T(8,128)}) custom-call(bf16[2,224,2560]{2,1,0:T(8,128)(2,1)} %get-tuple-element.29.g, f32[2,224,2560]{2,1,0:T(8,128)} %m.4, f32[2,224,2560]{2,1,0:T(8,128)} %v.4, bf16[2,896,2560]{2,1,0:T(8,128)(2,1)} %get-tuple-element.30.refs_0_), custom_call_target="tpu_custom_call" | custom-call | flops 38993920 | bytes 38993920 | tf_op jit(solution)/shard_map/pallas_call | solution.py:259
  450.9 0.0 copy-done.1
  450.9 17.9 %shard_map.187 = (bf16[2,896,2560]{2,1,0:T(8,128)(2,1)}, f32[2,224,2560]{2,1,0:T(8,128)}, f32[2,224,2560]{2,1,0:T(8,128)}) custom-call(bf16[2,224,2560]{2,1,0:T(8,128)(2,1)} %get-tuple-element.26.g, f32[2,224,2560]{2,1,0:T(8,128)} %m.3, f32[2,224,2560]{2,1,0:T(8,128)} %v.3, bf16[2,896,2560]{2,1,0:T(8,128)(2,1)} %get-tuple-element.27.refs_0_), custom_call_target="tpu_custom_call" | custom-call | flops 38993920 | bytes 38993920 | tf_op jit(solution)/shard_map/pallas_call | solution.py:259
  468.8 0.0 collective-permute-done.6.refs_10_
  468.8 0.0 copy-done
  468.8 3.3 collective-permute-start.11
  472.1 0.0 collective-permute-done.7.refs_11_
  472.1 5.8 %place.1 = bf16[2,2560,896]{2,1,0:T(8,128)(2,1)} custom-call(bf16[320,896]{1,0:T(8,128)(2,1)} %get-tuple-element.32.refs_0_, bf16[320,896]{1,0:T(8,128)(2,1)} %collective-permute-done.refs_1_, bf16[320,896]{1,0:T(8,128)(2,1)} %get-tuple-element.33.refs_2_, bf16[320,896]{1,0:T(8,128)(2,1)} %collective-permute-done.1.refs_3_, ...), custom_call_target="tpu_custom_call" | custom-call | flops 13762560 | bytes 13762560 | tf_op jit(solution)/shard_map/place/pallas_call | solution.py:234
  477.9 0.0 collective-permute-done.8
  477.9 0.9 bitcast_dynamic-update-slice_fusion.3
  478.8 0.0 collective-permute-done.9
  478.8 0.9 bitcast_dynamic-update-slice_fusion.2
  479.6 0.0 collective-permute-done.10
  479.6 0.9 bitcast_dynamic-update-slice_fusion.1
  480.5 0.0 collective-permute-done.11
  480.5 0.9 bitcast_dynamic-update-slice_fusion
Async XLA Ops:
  376.9 17.5 %collective-permute-start = (bf16[320,896]{1,0:T(8,128)(2,1)}, bf16[320,896]{1,0:T(8,128)(2,1)}, u32[]{:S(2)}, u32[]{:S(2)}) collective-permute-start(bf16[320,896]{1,0:T(8,128)(2,1)} %get-tuple-element.32.refs_0_), channel_id=1, source_target_pairs={{0,1},{1,2},{2,3},{3,0},{4,5},{5,6},{6,7},{7,4},{8,9},{9,10},{10,1... | collective-permute-start | bytes 1720328 | tf_op jit(solution)/shard_map/ppermute | solution.py:275
  378.3 16.2 %collective-permute-start.1 = (bf16[320,896]{1,0:T(8,128)(2,1)}, bf16[320,896]{1,0:T(8,128)(2,1)}, u32[]{:S(2)}, u32[]{:S(2)}) collective-permute-start(bf16[320,896]{1,0:T(8,128)(2,1)} %get-tuple-element.33.refs_2_), channel_id=1, source_target_pairs={{0,3},{1,0},{2,1},{3,2},{4,7},{5,4},{6,5},{7,6},{8,11},{9,8},{10,9... | collective-permute-start | bytes 1720328 | tf_op jit(solution)/shard_map/ppermute | solution.py:275
  380.2 26.3 %collective-permute-start.4 = (bf16[320,896]{1,0:T(8,128)(2,1)}, bf16[320,896]{1,0:T(8,128)(2,1)S(1)}, u32[]{:S(2)}, u32[]{:S(2)}) collective-permute-start(bf16[320,896]{1,0:T(8,128)(2,1)} %get-tuple-element.34.refs_6_), channel_id=1, source_target_pairs={{0,1},{1,2},{2,3},{3,0},{4,5},{5,6},{6,7},{7,4},{8,9},{9,10},{10,1... | collective-permute-start | bytes 1720328 | tf_op jit(solution)/shard_map/ppermute | solution.py:275
  380.4 26.3 %collective-permute-start.5 = (bf16[320,896]{1,0:T(8,128)(2,1)}, bf16[320,896]{1,0:T(8,128)(2,1)S(1)}, u32[]{:S(2)}, u32[]{:S(2)}) collective-permute-start(bf16[320,896]{1,0:T(8,128)(2,1)} %get-tuple-element.35.refs_8_), channel_id=1, source_target_pairs={{0,3},{1,0},{2,1},{3,2},{4,7},{5,4},{6,5},{7,6},{8,11},{9,8},{10,9... | collective-permute-start | bytes 1720328 | tf_op jit(solution)/shard_map/ppermute | solution.py:275
  383.5 35.6 %collective-permute-start.2 = (bf16[320,896]{1,0:T(8,128)(2,1)}, bf16[320,896]{1,0:T(8,128)(2,1)}, u32[]{:S(2)}, u32[]{:S(2)}) collective-permute-start(bf16[320,896]{1,0:T(8,128)(2,1)} %get-tuple-element.32.refs_0_), channel_id=1, source_target_pairs={{0,3},{1,0},{2,1},{3,2},{4,7},{5,4},{6,5},{7,6},{8,11},{9,8},{10,9... | collective-permute-start | bytes 1720328 | tf_op jit(solution)/shard_map/ppermute | solution.py:277
  394.4 27.8 %collective-permute-start.3 = (bf16[320,896]{1,0:T(8,128)(2,1)}, bf16[320,896]{1,0:T(8,128)(2,1)}, u32[]{:S(2)}, u32[]{:S(2)}) collective-permute-start(bf16[320,896]{1,0:T(8,128)(2,1)} %get-tuple-element.33.refs_2_), channel_id=1, source_target_pairs={{0,1},{1,2},{2,3},{3,0},{4,5},{5,6},{6,7},{7,4},{8,9},{9,10},{10,1... | collective-permute-start | bytes 1720328 | tf_op jit(solution)/shard_map/ppermute | solution.py:277
  394.5 74.3 %collective-permute-start.6 = (bf16[320,896]{1,0:T(8,128)(2,1)}, bf16[320,896]{1,0:T(8,128)(2,1)}, u32[]{:S(2)}, u32[]{:S(2)}) collective-permute-start(bf16[320,896]{1,0:T(8,128)(2,1)} %get-tuple-element.34.refs_6_), channel_id=1, source_target_pairs={{0,3},{1,0},{2,1},{3,2},{4,7},{5,4},{6,5},{7,6},{8,11},{9,8},{10,9... | collective-permute-start | bytes 1720328 | tf_op jit(solution)/shard_map/ppermute | solution.py:277
  406.6 44.4 %copy-start.1 = (bf16[320,896]{1,0:T(8,128)(2,1)}, bf16[320,896]{1,0:T(8,128)(2,1)S(1)}, u32[]{:S(2)}) copy-start(bf16[320,896]{1,0:T(8,128)(2,1)S(1)} %collective-permute-done.4.refs_7_) | copy-start | bytes 1720324
  406.6 65.6 %collective-permute-start.7 = (bf16[320,896]{1,0:T(8,128)(2,1)}, bf16[320,896]{1,0:T(8,128)(2,1)}, u32[]{:S(2)}, u32[]{:S(2)}) collective-permute-start(bf16[320,896]{1,0:T(8,128)(2,1)} %get-tuple-element.35.refs_8_), channel_id=1, source_target_pairs={{0,1},{1,2},{2,3},{3,0},{4,5},{5,6},{6,7},{7,4},{8,9},{9,10},{10,1... | collective-permute-start | bytes 1720328 | tf_op jit(solution)/shard_map/ppermute | solution.py:277
  406.7 62.1 %copy-start = (bf16[320,896]{1,0:T(8,128)(2,1)}, bf16[320,896]{1,0:T(8,128)(2,1)S(1)}, u32[]{:S(2)}) copy-start(bf16[320,896]{1,0:T(8,128)(2,1)S(1)} %collective-permute-done.5.refs_9_) | copy-start | bytes 1720324
  406.7 71.2 %collective-permute-start.8 = (bf16[320,896]{1,0:T(8,128)(2,1)}, bf16[320,896]{1,0:T(8,128)(2,1)S(1)}, u32[]{:S(2)}, u32[]{:S(2)}) collective-permute-start(bf16[320,896]{1,0:T(8,128)(2,1)} %collective-permute-done.refs_1_), channel_id=1, source_target_pairs={{0,1},{1,2},{2,3},{3,0},{4,5},{5,6},{6,7},{7,4},{8,9},{9,10},{10,1... | collective-permute-start | bytes 1720328 | tf_op jit(solution)/shard_map/ppermute | solution.py:280
  419.1 59.7 %collective-permute-start.9 = (bf16[320,896]{1,0:T(8,128)(2,1)}, bf16[320,896]{1,0:T(8,128)(2,1)S(1)}, u32[]{:S(2)}, u32[]{:S(2)}) collective-permute-start(bf16[320,896]{1,0:T(8,128)(2,1)} %collective-permute-done.1.refs_3_), channel_id=1, source_target_pairs={{0,3},{1,0},{2,1},{3,2},{4,7},{5,4},{6,5},{7,6},{8,11},{9,8},{10,9... | collective-permute-start | bytes 1720328 | tf_op jit(solution)/shard_map/ppermute | solution.py:280
  422.2 57.4 %collective-permute-start.10 = (bf16[320,896]{1,0:T(8,128)(2,1)S(1)}, bf16[320,896]{1,0:T(8,128)(2,1)S(1)}, u32[]{:S(2)}, u32[]{:S(2)}) collective-permute-start(bf16[320,896]{1,0:T(8,128)(2,1)S(1)} %collective-permute-done.4.refs_7_), channel_id=1, source_target_pairs={{0,1},{1,2},{2,3},{3,0},{4,5},{5,6},{6,7},{7,4},{8,9},{9,10},{10,1... | collective-permute-start | bytes 1720328 | tf_op jit(solution)/shard_map/ppermute | solution.py:280
  468.8 11.7 %collective-permute-start.11 = (bf16[320,896]{1,0:T(8,128)(2,1)S(1)}, bf16[320,896]{1,0:T(8,128)(2,1)S(1)}, u32[]{:S(2)}, u32[]{:S(2)}) collective-permute-start(bf16[320,896]{1,0:T(8,128)(2,1)S(1)} %collective-permute-done.5.refs_9_), channel_id=1, source_target_pairs={{0,3},{1,0},{2,1},{3,2},{4,7},{5,4},{6,5},{7,6},{8,11},{9,8},{10,9... | collective-permute-start | bytes 1720328 | tf_op jit(solution)/shard_map/ppermute | solution.py:280

commit v3 on v2

--- a/solution.py
+++ b/solution.py
@@ -13,7 +13,8 @@
 SENT = ("far_s", "far_r", "rel_s", "rel_r", "dir_s", "dir_r", "fwd_s", "fwd_r")
 LOCAL = ("term", "own", "w", "m", "v", "g_out", "w_out")
 BOTH_WAYS = ("near_s", "near_r")
-SEMAPHORES = (*SENT, *LOCAL, *BOTH_WAYS)
+SEMAPHORES = (*SENT, *LOCAL, *BOTH_WAYS, "again")
+LATER = 7
 
 
 def moments(m, v, g):
@@ -61,6 +62,15 @@
     for peer in (left, right):
         pl.semaphore_signal(barrier, inc=1, device_id={"dp": peer}, device_id_type=MESH)
     pl.semaphore_wait(barrier, 2)
+    late = lax.rem(lax.axis_index("rep"), 2)
+
+    def again(i, carry):
+        for peer in (left, right):
+            pl.semaphore_signal(sem["again"].at[lax.rem(i, 2)], inc=1, device_id={"dp": peer}, device_id_type=MESH)
+        pl.semaphore_wait(sem["again"].at[lax.rem(i, 2)], 2)
+        return carry
+
+    lax.fori_loop(0, LATER * late, again, 0)
 
     chunks = [(k, layer) for k in range(count) for layer in range(layers)]
     pending = []
@@ -192,7 +202,8 @@
     for w, piece, whole in zip(weights, pieces, gathered, strict=True):
         new += [jax.ShapeDtypeStruct(w.shape, BF16)] if whole else [jax.ShapeDtypeStruct(piece[2:], BF16)] * (2 * layers)
     out_shape = blocks + new
-    sems = [pltpu.SemaphoreType.DMA((chunks, 2, 2) if name in BOTH_WAYS else (chunks, 2)) for name in SEMAPHORES]
+    sems = [pltpu.SemaphoreType.DMA((chunks, 2, 2) if name in BOTH_WAYS else (chunks, 2)) for name in SEMAPHORES[:-1]]
+    sems.append(pltpu.SemaphoreType.REGULAR((2,)))
     return pl.pallas_call(
         functools.partial(kernel, n, layers, gathered),
         out_shape=out_shape,
@@ -242,28 +253,31 @@
     )(*pieces.values())
 
 
-def finish_kernel(g, m, v, *refs):
-    m_out, v_out = refs[-2:]
-    m_out[...], v_out[...] = moments(m[...], v[...], g[...].astype(F32))
-    if len(refs) > 2:
-        w, w_out = refs[:2]
-        w_out[...] = w[...]
-
-
-def finish(g, m, v, *w):
-    layers, depth, width = m.shape
-    steps = next(k for k in range(7, 0, -1) if depth % (16 * k) == 0)
-    block = pl.BlockSpec((1, depth // steps, width), lambda l, i: (l, i, 0))
-    whole = [pl.BlockSpec((1, one.shape[1] // steps, width), lambda l, i: (l, i, 0)) for one in w]
-    moved = m.size * 18 + sum(one.size * 4 for one in w)
+def carry_kernel(parts, src, out, buf, in_sem, out_sem):
+    layers, depth, _ = src.shape
+    spots = [(l, pl.ds(i * (depth // parts), depth // parts)) for l in range(layers) for i in range(parts)]
+    loads = [pltpu.make_async_copy(src.at[l, rows], buf.at[l, rows], in_sem.at[i]) for i, (l, rows) in enumerate(spots)]
+    stores = [pltpu.make_async_copy(buf.at[l, rows], out.at[l, rows], out_sem.at[i]) for i, (l, rows) in enumerate(spots)]
+    for load in loads:
+        load.start()
+    for load, store in zip(loads, stores, strict=True):
+        load.wait()
+        store.start()
+    for store in stores:
+        store.wait()
+
+
+def carry(w):
+    parts = next(k for k in range(8, 0, -1) if w.shape[1] % (16 * k) == 0)
+    moved = 4 * w.size
     return pl.pallas_call(
-        finish_kernel,
-        grid=(layers, steps),
-        out_shape=[jax.ShapeDtypeStruct(one.shape, BF16) for one in w] + [jax.ShapeDtypeStruct(m.shape, F32)] * 2,
-        in_specs=[block] * 3 + whole,
-        out_specs=whole + [block] * 2,
+        functools.partial(carry_kernel, parts),
+        out_shape=jax.ShapeDtypeStruct(w.shape, w.dtype),
+        in_specs=[pl.BlockSpec(memory_space=pl.ANY)],
+        out_specs=pl.BlockSpec(memory_space=pl.ANY),
+        scratch_shapes=[pltpu.VMEM(w.shape, w.dtype)] + [pltpu.SemaphoreType.DMA((w.shape[0] * parts,))] * 2,
         cost_estimate=pl.CostEstimate(flops=moved, bytes_accessed=moved, transcendentals=0),
-    )(g, m, v, *w)
+    )(w)
 
 
 def gather(n, shape, own):
@@ -296,14 +310,14 @@
         layers = m[0].shape[0]
         out = list(reduce_and_step(n, GATHERED, terms, weights, m, v))
         sums = [out.pop(0) for _ in range(3)]
-        new, m_new, v_new = [], [], []
+        new, pairs = [], []
         for k, whole in enumerate(GATHERED):
-            held = [out.pop(0)] if whole else []
-            *w, a, b = finish(sums[k], m[k], v[k], *held)
-            new.append(w[0] if whole else gather(n, weights[k].shape, [[out.pop(0) for _ in range(2)] for _ in range(layers)]))
-            m_new.append(a)
-            v_new.append(b)
-        return (*new, *m_new, *v_new)
+            pairs.append(moments(m[k], v[k], sums[k].astype(F32)))
+            if whole:
+                new.append(carry(out.pop(0)))
+            else:
+                new.append(gather(n, weights[k].shape, [[out.pop(0) for _ in range(2)] for _ in range(layers)]))
+        return (*new, *(one[0] for one in pairs), *(one[1] for one in pairs))
 
     all_of, cut = P(None, None, None), P(None, "dp", None)
     return jax.shard_map(

time: 483 us -> 452 us (0.936); the launches traced: 481 us -> 444 us
  Pallas kernels: 429 us -> 389 us
  other arithmetic: 0 us -> 20.9 us
  waiting for transfers between devices: 31.5 us -> 13.7 us
    pallas_call x3 -> x2, Pallas kernels: 46.6 us -> 14.5 us  [carry(): pl.pallas_call(functools.partial(carry_kernel, parts), out_shape=jax.Shap...]
    add x0 -> x2, other arithmetic: none -> 20.9 us  [moments(): return (0.9 * m + 0.1 * g, 0.95 * v + 0.05 * g * g)]
    ppermute x4, waiting for transfers between devices: 11.8 us -> 0.01 us  [gather(): lax.ppermute(sides[side], 'dp', behind)]
    ppermute x4, waiting for transfers between devices: 19.7 us -> 9.18 us  [gather(): near[layer, side, (n - 1, 1)[side]] = lax.ppermute(sides[side], 'dp', ahead)]
    pallas_call x1, Pallas kernels: 376 us -> 369 us  [reduce_and_step(): pl.pallas_call(functools.partial(kernel, n, layers, gathered), out_shape=...]
  transfers between devices with their start and end apart: 12 -> 12, of which waited for: 3 -> 4; matrix products, arithmetic and copies ran while one was open for 1% -> 5% of each run, Pallas kernels for 11% -> 5%
where the time goes in v3:
time: 452 us; the launch traced here: 444 us
  Pallas kernels  389 us (86%)
  other arithmetic  20.9 us (5%)
  starting transfers between devices  16.5 us (4%)
  waiting for transfers between devices  13.7 us (3%)
    pallas_call x1, Pallas kernels, reduce_and_step(): pl.pallas_call(functools.partial(kernel, n, layers, gathered), out_shape=...  369 us
    add x2, other arithmetic, moments(): return (0.9 * m + 0.1 * g, 0.95 * v + 0.05 * g * g)  20.9 us
    pallas_call x2, Pallas kernels, carry(): pl.pallas_call(functools.partial(carry_kernel, parts), out_shape=jax.Shap...  14.5 us
    ppermute x4, waiting for transfers between devices, gather(): near[layer, side, (n - 1, 1)[side]] = lax.ppermute(sides[side], 'dp', ahead)  9.18 us
  transfers between devices with their start and end apart: 12, of which 4 were waited for; matrix products, arithmetic and copies ran while one was open for 5% of the time, Pallas kernels for 5%

profile of v3, /device:TPU:112, one launch (start us, length us, event | category | flops | bytes accessed | tf_op | source)
XLA Modules:
  0.0 444.3 jit_solution(18246158965786863849)
XLA Ops:
  0.6 368.7 %reduce_and_step.1 = (bf16[2,224,2560]{2,1,0:T(8,128)(2,1)}, bf16[2,224,2560]{2,1,0:T(8,128)(2,1)}, bf16[2,640,896]{2,1,0:T(8,128)(2,1)}, bf16[2,896,2560]{2,1,0...) custom-call(bf16[1,2,896,2560]{3,2,1,0:T(8,128)(2,1)} %refs_0_.1, ...), custom_call_target="tpu_custom_call" | custom-call | tf_op jit(solution)/shard_map/reduce_and_step/pallas_call | solution.py:207
  369.4 2.7 collective-permute-start
  372.1 1.3 collective-permute-start.2
  373.4 1.9 collective-permute-start.1
  375.3 0.1 collective-permute-start.3
  375.4 0.7 collective-permute-start.4
  376.1 5.7 %collective-permute-done.refs_1_ = bf16[320,896]{1,0:T(8,128)(2,1)S(1)} collective-permute-done((bf16[320,896]{1,0:T(8,128)(2,1)}, bf16[320,896]{1,0:T(8,128)(2,1)S(1)}, u32[]{:S(2)}, u32[]{:S(2)}) %collective-permute-start) | collective-permute-done | bytes 573472 | tf_op jit(solution)/shard_map/ppermute | solution.py:289
  381.8 0.0 copy-start.3
  381.8 1.3 collective-permute-start.5
  383.2 0.0 copy-start.4
  383.2 0.0 copy-start
  383.2 0.0 copy-start.1
  383.2 0.0 copy-start.2
  383.2 15.9 %fusion.3 = (f32[2,224,2560]{2,1,0:T(8,128)}, f32[2,224,2560]{2,1,0:T(8,128)}, f32[2,224,2560]{2,1,0:T(8,128)}, f32[2,224,2560]{2,1,0:T(8,128)}) fusion(bf16[2,224,2560]{2,1,0:T(8,128)(2,1)} %get-tuple-element.24, f32[2,224,2560]{2,1,0:T(8,128)} %refs_9_.1, f32[2,224,2560]{2,1,0:T(8,128)} %refs_6_.1, bf16[2,224,2560]{2,1,0:T(8,128)(2,1)} %get-tuple-element.25, ...), kind=kLoop, calls=%fused_computation.9 | loop fusion | flops 18350080 | bytes 41287680 | tf_op jit(solution)/shard_map/add | solution.py:21
  399.1 0.0 collective-permute-done.1.refs_3_
  399.1 0.0 copy-done.4
  399.1 0.8 collective-permute-start.6
  399.9 0.0 collective-permute-done.2.refs_4_
  399.9 0.0 copy-start.5
  399.9 1.4 collective-permute-start.7
  401.3 0.0 copy-done.5
  401.3 0.0 collective-permute-done.3.refs_5_
  401.3 0.0 copy-done.3
  401.3 0.0 copy-start.6
  401.3 0.9 collective-permute-start.8
  402.2 0.0 copy-done.6
  402.2 3.4 collective-permute-done.4.refs_7_
  405.6 2.2 collective-permute-start.9
  407.8 0.0 collective-permute-done.5.refs_9_
  407.8 0.0 collective-permute-start.10
  407.8 0.0 copy-done
  407.8 0.0 copy-done.1
  407.8 0.0 copy-done.2
  407.8 4.9 %fusion.5 = (f32[2,640,896]{2,1,0:T(8,128)}, f32[2,640,896]{2,1,0:T(8,128)}) fusion(bf16[2,640,896]{2,1,0:T(8,128)(2,1)S(1)} %copy-done.2, f32[2,640,896]{2,1,0:T(8,128)S(1)} %copy-done.1, f32[2,640,896]{2,1,0:T(8,128)S(1)} %copy-done), kind=kLoop, calls=%fused_computation.11 | loop fusion | flops 9175040 | bytes 20643840 | tf_op jit(solution)/shard_map/add | solution.py:21
  412.8 7.2 %shard_map.187 = bf16[2,896,2560]{2,1,0:T(8,128)(2,1)} custom-call(bf16[2,896,2560]{2,1,0:T(8,128)(2,1)} %get-tuple-element.18.src), custom_call_target="tpu_custom_call" | custom-call | flops 18350080 | bytes 18350080 | tf_op jit(solution)/shard_map/pallas_call | solution.py:273
  420.0 7.2 %shard_map.188 = bf16[2,896,2560]{2,1,0:T(8,128)(2,1)} custom-call(bf16[2,896,2560]{2,1,0:T(8,128)(2,1)} %get-tuple-element.19.src), custom_call_target="tpu_custom_call" | custom-call | flops 18350080 | bytes 18350080 | tf_op jit(solution)/shard_map/pallas_call | solution.py:273
  427.3 0.0 collective-permute-done.6.refs_10_
  427.3 3.3 collective-permute-start.11
  430.6 0.0 collective-permute-done.7.refs_11_
  430.6 5.8 %place.1 = bf16[2,2560,896]{2,1,0:T(8,128)(2,1)} custom-call(bf16[320,896]{1,0:T(8,128)(2,1)} %get-tuple-element.20.refs_0_, bf16[320,896]{1,0:T(8,128)(2,1)} %copy-done.3, bf16[320,896]{1,0:T(8,128)(2,1)} %get-tuple-element.21.refs_2_, bf16[320,896]{1,0:T(8,128)(2,1)} %collective-permute-done.1.refs_3_, bf16[320,896]{1,0:T(8,128)(2,1)} %copy-done.5, ...), custom_call_target="tpu_custom_call" | custom-call | flops 13762560 | bytes 13762560 | tf_op jit(solution)/shard_map/place/pallas_call | solution.py:245
  436.3 0.0 collective-permute-done.8
  436.3 0.9 bitcast_dynamic-update-slice_fusion.3
  437.2 0.0 collective-permute-done.9
  437.2 0.9 bitcast_dynamic-update-slice_fusion.2
  438.1 4.3 collective-permute-done.10
  442.4 0.9 bitcast_dynamic-update-slice_fusion.1
  443.2 0.2 collective-permute-done.11
  443.4 0.9 bitcast_dynamic-update-slice_fusion
Async XLA Ops:
  369.4 12.5 %collective-permute-start = (bf16[320,896]{1,0:T(8,128)(2,1)}, bf16[320,896]{1,0:T(8,128)(2,1)S(1)}, u32[]{:S(2)}, u32[]{:S(2)}) collective-permute-start(bf16[320,896]{1,0:T(8,128)(2,1)} %get-tuple-element.20.refs_0_), channel_id=1, source_target_pairs={{0,1},{1,2},{2,3},{3,0},{4,5},{5,6},{6,7},{7,4},{8,9},{9,10},{10,1... | collective-permute-start | bytes 1720328 | tf_op jit(solution)/shard_map/ppermute | solution.py:289
  372.1 27.9 %collective-permute-start.2 = (bf16[320,896]{1,0:T(8,128)(2,1)}, bf16[320,896]{1,0:T(8,128)(2,1)S(1)}, u32[]{:S(2)}, u32[]{:S(2)}) collective-permute-start(bf16[320,896]{1,0:T(8,128)(2,1)} %get-tuple-element.20.refs_0_), channel_id=1, source_target_pairs={{0,3},{1,0},{2,1},{3,2},{4,7},{5,4},{6,5},{7,6},{8,11},{9,8},{10,9... | collective-permute-start | bytes 1720328 | tf_op jit(solution)/shard_map/ppermute | solution.py:291
  373.4 25.8 %collective-permute-start.1 = (bf16[320,896]{1,0:T(8,128)(2,1)}, bf16[320,896]{1,0:T(8,128)(2,1)}, u32[]{:S(2)}, u32[]{:S(2)}) collective-permute-start(bf16[320,896]{1,0:T(8,128)(2,1)} %get-tuple-element.21.refs_2_), channel_id=1, source_target_pairs={{0,3},{1,0},{2,1},{3,2},{4,7},{5,4},{6,5},{7,6},{8,11},{9,8},{10,9... | collective-permute-start | bytes 1720328 | tf_op jit(solution)/shard_map/ppermute | solution.py:289
  375.3 26.0 %collective-permute-start.3 = (bf16[320,896]{1,0:T(8,128)(2,1)}, bf16[320,896]{1,0:T(8,128)(2,1)S(1)}, u32[]{:S(2)}, u32[]{:S(2)}) collective-permute-start(bf16[320,896]{1,0:T(8,128)(2,1)} %get-tuple-element.21.refs_2_), channel_id=1, source_target_pairs={{0,1},{1,2},{2,3},{3,0},{4,5},{5,6},{6,7},{7,4},{8,9},{9,10},{10,1... | collective-permute-start | bytes 1720328 | tf_op jit(solution)/shard_map/ppermute | solution.py:291
  375.4 30.2 %collective-permute-start.4 = (bf16[320,896]{1,0:T(8,128)(2,1)}, bf16[320,896]{1,0:T(8,128)(2,1)}, u32[]{:S(2)}, u32[]{:S(2)}) collective-permute-start(bf16[320,896]{1,0:T(8,128)(2,1)} %get-tuple-element.22.refs_6_), channel_id=1, source_target_pairs={{0,1},{1,2},{2,3},{3,0},{4,5},{5,6},{6,7},{7,4},{8,9},{9,10},{10,1... | collective-permute-start | bytes 1720328 | tf_op jit(solution)/shard_map/ppermute | solution.py:289
  381.8 19.4 %copy-start.3 = (bf16[320,896]{1,0:T(8,128)(2,1)}, bf16[320,896]{1,0:T(8,128)(2,1)S(1)}, u32[]{:S(2)}) copy-start(bf16[320,896]{1,0:T(8,128)(2,1)S(1)} %collective-permute-done.refs_1_) | copy-start | bytes 1720324
  381.8 25.9 %collective-permute-start.5 = (bf16[320,896]{1,0:T(8,128)(2,1)}, bf16[320,896]{1,0:T(8,128)(2,1)}, u32[]{:S(2)}, u32[]{:S(2)}) collective-permute-start(bf16[320,896]{1,0:T(8,128)(2,1)} %get-tuple-element.23.refs_8_), channel_id=1, source_target_pairs={{0,3},{1,0},{2,1},{3,2},{4,7},{5,4},{6,5},{7,6},{8,11},{9,8},{10,9... | collective-permute-start | bytes 1720328 | tf_op jit(solution)/shard_map/ppermute | solution.py:289
  383.2 16.0 %copy-start.4 = (bf16[320,896]{1,0:T(8,128)(2,1)S(1)}, bf16[320,896]{1,0:T(8,128)(2,1)}, u32[]{:S(2)}) copy-start(bf16[320,896]{1,0:T(8,128)(2,1)} %get-tuple-element.22.refs_6_) | copy-start | bytes 1720324
  383.2 24.6 %copy-start = (f32[2,640,896]{2,1,0:T(8,128)S(1)}, f32[2,640,896]{2,1,0:T(8,128)}, u32[]{:S(2)}) copy-start(f32[2,640,896]{2,1,0:T(8,128)} %refs_8_.1) | copy-start | bytes 13762564
  383.2 24.6 %copy-start.1 = (f32[2,640,896]{2,1,0:T(8,128)S(1)}, f32[2,640,896]{2,1,0:T(8,128)}, u32[]{:S(2)}) copy-start(f32[2,640,896]{2,1,0:T(8,128)} %refs_11_.1) | copy-start | bytes 13762564
  383.2 24.6 %copy-start.2 = (bf16[2,640,896]{2,1,0:T(8,128)(2,1)S(1)}, bf16[2,640,896]{2,1,0:T(8,128)(2,1)}, u32[]{:S(2)}) copy-start(bf16[2,640,896]{2,1,0:T(8,128)(2,1)} %get-tuple-element.26) | copy-start | bytes 6881284
  399.1 28.1 %collective-permute-start.6 = (bf16[320,896]{1,0:T(8,128)(2,1)S(1)}, bf16[320,896]{1,0:T(8,128)(2,1)}, u32[]{:S(2)}, u32[]{:S(2)}) collective-permute-start(bf16[320,896]{1,0:T(8,128)(2,1)S(1)} %copy-done.4), channel_id=1, source_target_pairs={{0,3},{1,0},{2,1},{3,2},{4,7},{5,4},{6,5},{7,6},{8,11},{9,8},{10,9... | collective-permute-start | bytes 1720328 | tf_op jit(solution)/shard_map/ppermute | solution.py:291
  399.9 1.4 copy-start.5
  399.9 30.7 %collective-permute-start.7 = (bf16[320,896]{1,0:T(8,128)(2,1)}, bf16[320,896]{1,0:T(8,128)(2,1)}, u32[]{:S(2)}, u32[]{:S(2)}) collective-permute-start(bf16[320,896]{1,0:T(8,128)(2,1)} %get-tuple-element.23.refs_8_), channel_id=1, source_target_pairs={{0,1},{1,2},{2,3},{3,0},{4,5},{5,6},{6,7},{7,4},{8,9},{9,10},{10,1... | collective-permute-start | bytes 1720328 | tf_op jit(solution)/shard_map/ppermute | solution.py:291
  401.3 0.9 copy-start.6
  401.3 35.0 %collective-permute-start.8 = (bf16[320,896]{1,0:T(8,128)(2,1)S(1)}, bf16[320,896]{1,0:T(8,128)(2,1)S(1)}, u32[]{:S(2)}, u32[]{:S(2)}) collective-permute-start(bf16[320,896]{1,0:T(8,128)(2,1)S(1)} %collective-permute-done.refs_1_), channel_id=1, source_target_pairs={{0,1},{1,2},{2,3},{3,0},{4,5},{5,6},{6,7},{7,4},{8,9},{9,10},{10,1... | collective-permute-start | bytes 1720328 | tf_op jit(solution)/shard_map/ppermute | solution.py:294
  405.6 31.6 %collective-permute-start.9 = (bf16[320,896]{1,0:T(8,128)(2,1)}, bf16[320,896]{1,0:T(8,128)(2,1)S(1)}, u32[]{:S(2)}, u32[]{:S(2)}) collective-permute-start(bf16[320,896]{1,0:T(8,128)(2,1)} %collective-permute-done.1.refs_3_), channel_id=1, source_target_pairs={{0,3},{1,0},{2,1},{3,2},{4,7},{5,4},{6,5},{7,6},{8,11},{9,8},{10,9... | collective-permute-start | bytes 1720328 | tf_op jit(solution)/shard_map/ppermute | solution.py:294
  407.8 34.6 %collective-permute-start.10 = (bf16[320,896]{1,0:T(8,128)(2,1)}, bf16[320,896]{1,0:T(8,128)(2,1)S(1)}, u32[]{:S(2)}, u32[]{:S(2)}) collective-permute-start(bf16[320,896]{1,0:T(8,128)(2,1)} %collective-permute-done.4.refs_7_), channel_id=1, source_target_pairs={{0,1},{1,2},{2,3},{3,0},{4,5},{5,6},{6,7},{7,4},{8,9},{9,10},{10,1... | collective-permute-start | bytes 1720328 | tf_op jit(solution)/shard_map/ppermute | solution.py:294
  427.3 16.1 %collective-permute-start.11 = (bf16[320,896]{1,0:T(8,128)(2,1)}, bf16[320,896]{1,0:T(8,128)(2,1)S(1)}, u32[]{:S(2)}, u32[]{:S(2)}) collective-permute-start(bf16[320,896]{1,0:T(8,128)(2,1)} %collective-permute-done.5.refs_9_), channel_id=1, source_target_pairs={{0,3},{1,0},{2,1},{3,2},{4,7},{5,4},{6,5},{7,6},{8,11},{9,8},{10,9... | collective-permute-start | bytes 1720328 | tf_op jit(solution)/shard_map/ppermute | solution.py:294

commit v4 on v3

--- a/solution.py
+++ b/solution.py
@@ -14,7 +14,7 @@
 LOCAL = ("term", "own", "w", "m", "v", "g_out", "w_out")
 BOTH_WAYS = ("near_s", "near_r")
 SEMAPHORES = (*SENT, *LOCAL, *BOTH_WAYS, "again")
-LATER = 7
+LATER = 6
 
 
 def moments(m, v, g):
@@ -62,7 +62,7 @@
     for peer in (left, right):
         pl.semaphore_signal(barrier, inc=1, device_id={"dp": peer}, device_id_type=MESH)
     pl.semaphore_wait(barrier, 2)
-    late = lax.rem(lax.axis_index("rep"), 2)
+    late = 1 - lax.rem(lax.axis_index("rep"), 2)
 
     def again(i, carry):
         for peer in (left, right):
@@ -253,11 +253,15 @@
     )(*pieces.values())
 
 
-def carry_kernel(parts, src, out, buf, in_sem, out_sem):
-    layers, depth, _ = src.shape
-    spots = [(l, pl.ds(i * (depth // parts), depth // parts)) for l in range(layers) for i in range(parts)]
-    loads = [pltpu.make_async_copy(src.at[l, rows], buf.at[l, rows], in_sem.at[i]) for i, (l, rows) in enumerate(spots)]
-    stores = [pltpu.make_async_copy(buf.at[l, rows], out.at[l, rows], out_sem.at[i]) for i, (l, rows) in enumerate(spots)]
+def carry_kernel(parts, *refs):
+    count = (len(refs) - 2) // 3
+    src, out, buf = (refs[i * count : (i + 1) * count] for i in range(3))
+    in_sem, out_sem = refs[3 * count :]
+    layers, depth, _ = src[0].shape
+    rows = depth // parts
+    spots = [(k, l, pl.ds(i * rows, rows)) for k in range(count) for l in range(layers) for i in range(parts)]
+    loads = [pltpu.make_async_copy(src[k].at[l, here], buf[k].at[l, here], in_sem.at[i]) for i, (k, l, here) in enumerate(spots)]
+    stores = [pltpu.make_async_copy(buf[k].at[l, here], out[k].at[l, here], out_sem.at[i]) for i, (k, l, here) in enumerate(spots)]
     for load in loads:
         load.start()
     for load, store in zip(loads, stores, strict=True):
@@ -267,17 +271,19 @@
         store.wait()
 
 
-def carry(w):
+def carry(arrays):
+    w, count = arrays[0], len(arrays)
     parts = next(k for k in range(8, 0, -1) if w.shape[1] % (16 * k) == 0)
-    moved = 4 * w.size
+    moved = 4 * w.size * count
     return pl.pallas_call(
         functools.partial(carry_kernel, parts),
-        out_shape=jax.ShapeDtypeStruct(w.shape, w.dtype),
-        in_specs=[pl.BlockSpec(memory_space=pl.ANY)],
-        out_specs=pl.BlockSpec(memory_space=pl.ANY),
-        scratch_shapes=[pltpu.VMEM(w.shape, w.dtype)] + [pltpu.SemaphoreType.DMA((w.shape[0] * parts,))] * 2,
+        out_shape=[jax.ShapeDtypeStruct(w.shape, w.dtype)] * count,
+        in_specs=[pl.BlockSpec(memory_space=pl.ANY)] * count,
+        out_specs=[pl.BlockSpec(memory_space=pl.ANY)] * count,
+        scratch_shapes=[pltpu.VMEM(w.shape, w.dtype)] * count + [pltpu.SemaphoreType.DMA((count * w.shape[0] * parts,))] * 2,
         cost_estimate=pl.CostEstimate(flops=moved, bytes_accessed=moved, transcendentals=0),
-    )(w)
+        name="carry",
+    )(*arrays)
 
 
 def gather(n, shape, own):
@@ -292,10 +298,12 @@
     for layer, sides in enumerate(own):
         for side, ahead in enumerate((right, left)):
             far[layer, side] = lax.ppermute(near[layer, side, (n - 1, 1)[side]], "dp", ahead)
-    whole = place(n, shape, near)
+    early = {(layer, side, 2): far[layer, side] for layer in range(len(own) - 1) for side in (0, 1)}
+    whole = place(n, shape, {**near, **early})
     opposite = lax.rem(lax.axis_index("dp") + 2, n)
-    for (layer, side), piece in far.items():
-        whole = lax.dynamic_update_slice(whole, piece[None], (layer, (2 * opposite + side) * piece.shape[0], 0))
+    for side in (0, 1):
+        piece = far[len(own) - 1, side]
+        whole = lax.dynamic_update_slice(whole, piece[None], (len(own) - 1, (2 * opposite + side) * piece.shape[0], 0))
     return whole
 
 
@@ -310,13 +318,14 @@
         layers = m[0].shape[0]
         out = list(reduce_and_step(n, GATHERED, terms, weights, m, v))
         sums = [out.pop(0) for _ in range(3)]
-        new, pairs = [], []
+        held, new, pairs = [], [], []
         for k, whole in enumerate(GATHERED):
             pairs.append(moments(m[k], v[k], sums[k].astype(F32)))
             if whole:
-                new.append(carry(out.pop(0)))
+                held.append(out.pop(0))
             else:
                 new.append(gather(n, weights[k].shape, [[out.pop(0) for _ in range(2)] for _ in range(layers)]))
+        new = [*carry(held), *new]
         return (*new, *(one[0] for one in pairs), *(one[1] for one in pairs))
 
     all_of, cut = P(None, None, None), P(None, "dp", None)

time: 452 us -> 465 us (1.029); the launches traced: 444 us -> 465 us
  waiting for transfers between devices: 13.7 us -> 26.2 us
  Pallas kernels: 389 us -> 400 us
    ppermute x4, waiting for transfers between devices: 9.18 us -> 26.1 us  [gather(): near[layer, side, (n - 1, 1)[side]] = lax.ppermute(sides[side], 'dp', ahead)]
    pallas_call x1, Pallas kernels: 369 us -> 381 us  [reduce_and_step(): pl.pallas_call(functools.partial(kernel, n, layers, gathered), out_shape=...]
    pallas_call x2 -> x1, Pallas kernels: 14.5 us -> 13.1 us  [carry(): pl.pallas_call(functools.partial(carry_kernel, parts), out_shape=[jax.Sha...]
  transfers between devices with their start and end apart: 12 -> 12, of which waited for: 4 -> 4; matrix products, arithmetic and copies ran while one was open for 5% -> 5% of each run, Pallas kernels for 5% -> 4%
where the time goes in v4:
time: 465 us
  Pallas kernels  400 us (86%)
  waiting for transfers between devices  26.2 us (6%)
  other arithmetic  20.9 us (4%)
  starting transfers between devices  15.4 us (3%)
    pallas_call x1, Pallas kernels, reduce_and_step(): pl.pallas_call(functools.partial(kernel, n, layers, gathered), out_shape=...  381 us
    ppermute x4, waiting for transfers between devices, gather(): near[layer, side, (n - 1, 1)[side]] = lax.ppermute(sides[side], 'dp', ahead)  26.1 us
    add x2, other arithmetic, moments(): return (0.9 * m + 0.1 * g, 0.95 * v + 0.05 * g * g)  20.9 us
    pallas_call x1, Pallas kernels, carry(): pl.pallas_call(functools.partial(carry_kernel, parts), out_shape=[jax.Sha...  13.1 us
  transfers between devices with their start and end apart: 12, of which 4 were waited for; matrix products, arithmetic and copies ran while one was open for 5% of the time, Pallas kernels for 4%

profile of v4, /device:TPU:112, one launch (start us, length us, event | category | flops | bytes accessed | tf_op | source)
XLA Modules:
  0.0 464.8 jit_solution(2092026197367943750)
XLA Ops:
  0.6 380.6 %reduce_and_step.1 = (bf16[2,224,2560]{2,1,0:T(8,128)(2,1)}, bf16[2,224,2560]{2,1,0:T(8,128)(2,1)}, bf16[2,640,896]{2,1,0:T(8,128)(2,1)}, bf16[2,896,2560]{2,1,0...) custom-call(bf16[1,2,896,2560]{3,2,1,0:T(8,128)(2,1)} %refs_0_.1, ...), custom_call_target="tpu_custom_call" | custom-call | tf_op jit(solution)/shard_map/reduce_and_step/pallas_call | solution.py:207
  381.3 2.6 collective-permute-start
  383.9 0.7 collective-permute-start.1
  384.6 0.9 collective-permute-start.2
  385.5 1.1 collective-permute-start.3
  386.6 1.3 collective-permute-start.4
  388.0 10.7 %collective-permute-done.refs_1_ = bf16[320,896]{1,0:T(8,128)(2,1)S(1)} collective-permute-done((bf16[320,896]{1,0:T(8,128)(2,1)}, bf16[320,896]{1,0:T(8,128)(2,1)S(1)}, u32[]{:S(2)}, u32[]{:S(2)}) %collective-permute-start) | collective-permute-done | bytes 573472 | tf_op jit(solution)/shard_map/ppermute | solution.py:295
  398.6 0.0 copy-start.4
  398.6 0.9 collective-permute-start.6
  399.6 0.4 collective-permute-done.1.refs_3_
  400.0 0.0 copy-start.5
  400.0 1.9 collective-permute-start.5
  401.9 0.0 copy-start.3
  401.9 0.0 copy-start
  401.9 0.0 copy-start.1
  401.9 0.0 copy-start.2
  401.9 15.9 %fusion.3 = (f32[2,224,2560]{2,1,0:T(8,128)}, f32[2,224,2560]{2,1,0:T(8,128)}, f32[2,224,2560]{2,1,0:T(8,128)}, f32[2,224,2560]{2,1,0:T(8,128)}) fusion(bf16[2,224,2560]{2,1,0:T(8,128)(2,1)} %get-tuple-element.28, f32[2,224,2560]{2,1,0:T(8,128)} %refs_9_.1, f32[2,224,2560]{2,1,0:T(8,128)} %refs_6_.1, bf16[2,224,2560]{2,1,0:T(8,128)(2,1)} %get-tuple-element.29, ...), kind=kLoop, calls=%fused_computation.9 | loop fusion | flops 18350080 | bytes 41287680 | tf_op jit(solution)/shard_map/add | solution.py:21
  417.8 0.0 collective-permute-done.2.refs_4_
  417.8 0.0 copy-done.3
  417.9 0.0 copy-start.6
  417.9 0.2 collective-permute-start.7
  418.1 0.0 collective-permute-done.3.refs_5_
  418.1 0.0 copy-done.4
  418.1 0.7 collective-permute-start.8
  418.8 2.5 collective-permute-done.4.refs_7_
  421.3 0.0 copy-done.5
  421.3 0.0 copy-start.7
  421.3 1.7 collective-permute-start.9
  423.0 0.0 copy-done.7
  423.0 12.6 %collective-permute-done.5.refs_9_ = bf16[320,896]{1,0:T(8,128)(2,1)} collective-permute-done((bf16[320,896]{1,0:T(8,128)(2,1)}, bf16[320,896]{1,0:T(8,128)(2,1)}, u32[]{:S(2)}, u32[]{:S(2)}) %collective-permute-start.5) | collective-permute-done | bytes 573472 | tf_op jit(solution)/shard_map/ppermute | solution.py:295
  435.6 1.3 collective-permute-start.10
  436.9 0.0 copy-done.6
  436.9 0.0 collective-permute-done.6.refs_10_
  436.9 1.9 collective-permute-start.11
  438.8 0.0 copy-done
  438.8 0.0 copy-done.1
  438.8 0.0 copy-done.2
  438.8 4.9 %fusion.5 = (f32[2,640,896]{2,1,0:T(8,128)}, f32[2,640,896]{2,1,0:T(8,128)}) fusion(bf16[2,640,896]{2,1,0:T(8,128)(2,1)S(1)} %copy-done.2, f32[2,640,896]{2,1,0:T(8,128)S(1)} %copy-done.1, f32[2,640,896]{2,1,0:T(8,128)S(1)} %copy-done), kind=kLoop, calls=%fused_computation.11 | loop fusion | flops 9175040 | bytes 20643840 | tf_op jit(solution)/shard_map/add | solution.py:21
  443.8 13.1 %carry.1 = (bf16[2,896,2560]{2,1,0:T(8,128)(2,1)}, bf16[2,896,2560]{2,1,0:T(8,128)(2,1)}) custom-call(bf16[2,896,2560]{2,1,0:T(8,128)(2,1)} %get-tuple-element.20.refs_0_, bf16[2,896,2560]{2,1,0:T(8,128)(2,1)} %get-tuple-element.21.refs_1_), custom_call_target="tpu_custom_call" | custom-call | flops 36700160 | bytes 36700160 | tf_op jit(solution)/shard_map/carry/pallas_call | solution.py:278
  456.8 0.0 collective-permute-done.7.refs_11_
  456.8 0.0 collective-permute-done.8.refs_12_
  456.9 0.0 collective-permute-done.9.refs_13_
  456.9 6.2 %place.1 = bf16[2,2560,896]{2,1,0:T(8,128)(2,1)} custom-call(bf16[320,896]{1,0:T(8,128)(2,1)} %get-tuple-element.24.refs_0_, bf16[320,896]{1,0:T(8,128)(2,1)} %copy-done.4, bf16[320,896]{1,0:T(8,128)(2,1)} %get-tuple-element.25.refs_2_, bf16[320,896]{1,0:T(8,128)(2,1)} %copy-done.5, bf16[320,896]{1,0:T(8,128)(2,1)} %copy-done.6, ...), custom_call_target="tpu_custom_call" | custom-call | flops 16056320 | bytes 16056320 | tf_op jit(solution)/shard_map/place/pallas_call | solution.py:245
  463.1 0.0 collective-permute-done.10
  463.1 0.9 bitcast_dynamic-update-slice_fusion.1
  463.9 0.0 collective-permute-done.11
  463.9 0.9 bitcast_dynamic-update-slice_fusion
Async XLA Ops:
  381.3 17.3 %collective-permute-start = (bf16[320,896]{1,0:T(8,128)(2,1)}, bf16[320,896]{1,0:T(8,128)(2,1)S(1)}, u32[]{:S(2)}, u32[]{:S(2)}) collective-permute-start(bf16[320,896]{1,0:T(8,128)(2,1)} %get-tuple-element.24.refs_0_), channel_id=1, source_target_pairs={{0,1},{1,2},{2,3},{3,0},{4,5},{5,6},{6,7},{7,4},{8,9},{9,10},{10,1... | collective-permute-start | bytes 1720328 | tf_op jit(solution)/shard_map/ppermute | solution.py:295
  383.9 16.1 %collective-permute-start.1 = (bf16[320,896]{1,0:T(8,128)(2,1)}, bf16[320,896]{1,0:T(8,128)(2,1)S(1)}, u32[]{:S(2)}, u32[]{:S(2)}) collective-permute-start(bf16[320,896]{1,0:T(8,128)(2,1)} %get-tuple-element.25.refs_2_), channel_id=1, source_target_pairs={{0,3},{1,0},{2,1},{3,2},{4,7},{5,4},{6,5},{7,6},{8,11},{9,8},{10,9... | collective-permute-start | bytes 1720328 | tf_op jit(solution)/shard_map/ppermute | solution.py:295
  384.6 33.2 %collective-permute-start.2 = (bf16[320,896]{1,0:T(8,128)(2,1)}, bf16[320,896]{1,0:T(8,128)(2,1)S(1)}, u32[]{:S(2)}, u32[]{:S(2)}) collective-permute-start(bf16[320,896]{1,0:T(8,128)(2,1)} %get-tuple-element.24.refs_0_), channel_id=1, source_target_pairs={{0,3},{1,0},{2,1},{3,2},{4,7},{5,4},{6,5},{7,6},{8,11},{9,8},{10,9... | collective-permute-start | bytes 1720328 | tf_op jit(solution)/shard_map/ppermute | solution.py:297
  385.5 32.5 %collective-permute-start.3 = (bf16[320,896]{1,0:T(8,128)(2,1)}, bf16[320,896]{1,0:T(8,128)(2,1)}, u32[]{:S(2)}, u32[]{:S(2)}) collective-permute-start(bf16[320,896]{1,0:T(8,128)(2,1)} %get-tuple-element.25.refs_2_), channel_id=1, source_target_pairs={{0,1},{1,2},{2,3},{3,0},{4,5},{5,6},{6,7},{7,4},{8,9},{9,10},{10,1... | collective-permute-start | bytes 1720328 | tf_op jit(solution)/shard_map/ppermute | solution.py:297
  386.6 34.6 %collective-permute-start.4 = (bf16[320,896]{1,0:T(8,128)(2,1)}, bf16[320,896]{1,0:T(8,128)(2,1)S(1)}, u32[]{:S(2)}, u32[]{:S(2)}) collective-permute-start(bf16[320,896]{1,0:T(8,128)(2,1)} %get-tuple-element.26.refs_6_), channel_id=1, source_target_pairs={{0,1},{1,2},{2,3},{3,0},{4,5},{5,6},{6,7},{7,4},{8,9},{9,10},{10,1... | collective-permute-start | bytes 1720328 | tf_op jit(solution)/shard_map/ppermute | solution.py:295
  398.6 19.4 %copy-start.4 = (bf16[320,896]{1,0:T(8,128)(2,1)}, bf16[320,896]{1,0:T(8,128)(2,1)S(1)}, u32[]{:S(2)}) copy-start(bf16[320,896]{1,0:T(8,128)(2,1)S(1)} %collective-permute-done.refs_1_) | copy-start | bytes 1720324
  398.6 38.2 %collective-permute-start.6 = (bf16[320,896]{1,0:T(8,128)(2,1)}, bf16[320,896]{1,0:T(8,128)(2,1)}, u32[]{:S(2)}, u32[]{:S(2)}) collective-permute-start(bf16[320,896]{1,0:T(8,128)(2,1)} %get-tuple-element.26.refs_6_), channel_id=1, source_target_pairs={{0,3},{1,0},{2,1},{3,2},{4,7},{5,4},{6,5},{7,6},{8,11},{9,8},{10,9... | collective-permute-start | bytes 1720328 | tf_op jit(solution)/shard_map/ppermute | solution.py:297
  400.0 21.3 %copy-start.5 = (bf16[320,896]{1,0:T(8,128)(2,1)}, bf16[320,896]{1,0:T(8,128)(2,1)S(1)}, u32[]{:S(2)}) copy-start(bf16[320,896]{1,0:T(8,128)(2,1)S(1)} %collective-permute-done.1.refs_3_) | copy-start | bytes 1720324
  400.0 35.6 %collective-permute-start.5 = (bf16[320,896]{1,0:T(8,128)(2,1)}, bf16[320,896]{1,0:T(8,128)(2,1)}, u32[]{:S(2)}, u32[]{:S(2)}) collective-permute-start(bf16[320,896]{1,0:T(8,128)(2,1)} %get-tuple-element.27.refs_8_), channel_id=1, source_target_pairs={{0,3},{1,0},{2,1},{3,2},{4,7},{5,4},{6,5},{7,6},{8,11},{9,8},{10,9... | collective-permute-start | bytes 1720328 | tf_op jit(solution)/shard_map/ppermute | solution.py:295
  401.9 16.0 %copy-start.3 = (bf16[320,896]{1,0:T(8,128)(2,1)S(1)}, bf16[320,896]{1,0:T(8,128)(2,1)}, u32[]{:S(2)}) copy-start(bf16[320,896]{1,0:T(8,128)(2,1)} %get-tuple-element.27.refs_8_) | copy-start | bytes 1720324
  401.9 36.9 %copy-start = (f32[2,640,896]{2,1,0:T(8,128)S(1)}, f32[2,640,896]{2,1,0:T(8,128)}, u32[]{:S(2)}) copy-start(f32[2,640,896]{2,1,0:T(8,128)} %refs_8_.1) | copy-start | bytes 13762564
  401.9 36.9 %copy-start.1 = (f32[2,640,896]{2,1,0:T(8,128)S(1)}, f32[2,640,896]{2,1,0:T(8,128)}, u32[]{:S(2)}) copy-start(f32[2,640,896]{2,1,0:T(8,128)} %refs_11_.1) | copy-start | bytes 13762564
  401.9 36.9 %copy-start.2 = (bf16[2,640,896]{2,1,0:T(8,128)(2,1)S(1)}, bf16[2,640,896]{2,1,0:T(8,128)(2,1)}, u32[]{:S(2)}) copy-start(bf16[2,640,896]{2,1,0:T(8,128)(2,1)} %get-tuple-element.30) | copy-start | bytes 6881284
  417.9 19.0 %copy-start.6 = (bf16[320,896]{1,0:T(8,128)(2,1)}, bf16[320,896]{1,0:T(8,128)(2,1)S(1)}, u32[]{:S(2)}) copy-start(bf16[320,896]{1,0:T(8,128)(2,1)S(1)} %collective-permute-done.2.refs_4_) | copy-start | bytes 1720324
  417.9 39.0 %collective-permute-start.7 = (bf16[320,896]{1,0:T(8,128)(2,1)S(1)}, bf16[320,896]{1,0:T(8,128)(2,1)}, u32[]{:S(2)}, u32[]{:S(2)}) collective-permute-start(bf16[320,896]{1,0:T(8,128)(2,1)S(1)} %copy-done.3), channel_id=1, source_target_pairs={{0,1},{1,2},{2,3},{3,0},{4,5},{5,6},{6,7},{7,4},{8,9},{9,10},{10,1... | collective-permute-start | bytes 1720328 | tf_op jit(solution)/shard_map/ppermute | solution.py:297
  418.1 38.8 %collective-permute-start.8 = (bf16[320,896]{1,0:T(8,128)(2,1)S(1)}, bf16[320,896]{1,0:T(8,128)(2,1)}, u32[]{:S(2)}, u32[]{:S(2)}) collective-permute-start(bf16[320,896]{1,0:T(8,128)(2,1)S(1)} %collective-permute-done.refs_1_), channel_id=1, source_target_pairs={{0,1},{1,2},{2,3},{3,0},{4,5},{5,6},{6,7},{7,4},{8,9},{9,10},{10,1... | collective-permute-start | bytes 1720328 | tf_op jit(solution)/shard_map/ppermute | solution.py:300
  421.3 1.7 copy-start.7
  421.3 35.6 %collective-permute-start.9 = (bf16[320,896]{1,0:T(8,128)(2,1)S(1)}, bf16[320,896]{1,0:T(8,128)(2,1)}, u32[]{:S(2)}, u32[]{:S(2)}) collective-permute-start(bf16[320,896]{1,0:T(8,128)(2,1)S(1)} %collective-permute-done.1.refs_3_), channel_id=1, source_target_pairs={{0,3},{1,0},{2,1},{3,2},{4,7},{5,4},{6,5},{7,6},{8,11},{9,8},{10,9... | collective-permute-start | bytes 1720328 | tf_op jit(solution)/shard_map/ppermute | solution.py:300
  435.6 27.5 %collective-permute-start.10 = (bf16[320,896]{1,0:T(8,128)(2,1)}, bf16[320,896]{1,0:T(8,128)(2,1)S(1)}, u32[]{:S(2)}, u32[]{:S(2)}) collective-permute-start(bf16[320,896]{1,0:T(8,128)(2,1)} %copy-done.7), channel_id=1, source_target_pairs={{0,1},{1,2},{2,3},{3,0},{4,5},{5,6},{6,7},{7,4},{8,9},{9,10},{10,1... | collective-permute-start | bytes 1720328 | tf_op jit(solution)/shard_map/ppermute | solution.py:300
  436.9 27.0 %collective-permute-start.11 = (bf16[320,896]{1,0:T(8,128)(2,1)}, bf16[320,896]{1,0:T(8,128)(2,1)S(1)}, u32[]{:S(2)}, u32[]{:S(2)}) collective-permute-start(bf16[320,896]{1,0:T(8,128)(2,1)} %collective-permute-done.5.refs_9_), channel_id=1, source_target_pairs={{0,3},{1,0},{2,1},{3,2},{4,7},{5,4},{6,5},{7,6},{8,11},{9,8},{10,9... | collective-permute-start | bytes 1720328 | tf_op jit(solution)/shard_map/ppermute | solution.py:300

commit v5 on v4

--- a/solution.py
+++ b/solution.py
@@ -11,10 +11,10 @@
 MESH = pl.DeviceIdType.MESH
 BF16, F32 = jnp.bfloat16, jnp.float32
 SENT = ("far_s", "far_r", "rel_s", "rel_r", "dir_s", "dir_r", "fwd_s", "fwd_r")
-LOCAL = ("term", "own", "w", "m", "v", "g_out", "w_out")
-BOTH_WAYS = ("near_s", "near_r")
+LOCAL = ("term", "own", "w", "m", "v", "g_out")
+BOTH_WAYS = ("near_s", "near_r", "w_out")
 SEMAPHORES = (*SENT, *LOCAL, *BOTH_WAYS, "again")
-LATER = 6
+LATER = 5
 
 
 def moments(m, v, g):
@@ -30,6 +30,11 @@
     while width % (parts * 128):
         parts += 1
     return [slice(i * (width // parts), (i + 1) * (width // parts)) for i in range(parts)]
+
+
+def cuts(half):
+    last = max(16, half // 5 // 16 * 16)
+    return (0, half - last), (half - last, last)
 
 
 def tiled(shape, body):
@@ -48,7 +53,7 @@
     take = lambda k: [refs.pop(0) for _ in range(k)]
     g, w, m, v = take(count), take(count), take(count), take(count)
     g_out = take(count)
-    w_out = [take(1)[0] if whole else [[refs.pop(0) for _ in range(2)] for _ in range(layers)] for whole in gathered]
+    w_out = [take(1)[0] if whole else [take(2) for _ in cuts(w[k].shape[1] // (2 * n))] for k, whole in enumerate(gathered)]
     far, rel, direct, term, own, new = (take(count) for _ in range(6))
     m_buf, v_buf = take(count), take(count)
     sem = dict(zip(SEMAPHORES, refs, strict=True))
@@ -156,9 +161,10 @@
                 place = w_out[k].at[l, rows(k, me, side)]
                 for way, peer in enumerate((ahead[side], behind[side])):
                     sent["near", c, side, way] = send(x, place, sem["near_s"].at[c, side, way], sem["near_r"].at[c, side, way], peer)
+                pending.append(local(x, place, sem["w_out"].at[c, side, 0]).wait)
             else:
-                place = w_out[k][l][side]
-            pending.append(local(x, place, sem["w_out"].at[c, side]).wait)
+                for i, (start, size) in enumerate(cuts(half)):
+                    pending.append(local(x.at[pl.ds(start, size)], w_out[k][i][side].at[l], sem["w_out"].at[c, side, i]).wait)
             if c + 1 < len(chunks):
                 load_moments(c + 1, side)
 
@@ -200,7 +206,10 @@
     blocks = [jax.ShapeDtypeStruct(one.shape, BF16) for one in m]
     new = []
     for w, piece, whole in zip(weights, pieces, gathered, strict=True):
-        new += [jax.ShapeDtypeStruct(w.shape, BF16)] if whole else [jax.ShapeDtypeStruct(piece[2:], BF16)] * (2 * layers)
+        if whole:
+            new.append(jax.ShapeDtypeStruct(w.shape, BF16))
+        else:
+            new += [jax.ShapeDtypeStruct((layers, size, piece[3]), BF16) for _, size in cuts(piece[2]) for _ in range(2)]
     out_shape = blocks + new
     sems = [pltpu.SemaphoreType.DMA((chunks, 2, 2) if name in BOTH_WAYS else (chunks, 2)) for name in SEMAPHORES[:-1]]
     sems.append(pltpu.SemaphoreType.REGULAR((2,)))
@@ -218,20 +227,21 @@
 
 
 def place_kernel(n, spots, *refs):
-    pieces = refs[: len(spots)]
-    out, buf, in_sem, out_sem = refs[len(spots) :]
+    count = len(spots)
+    pieces, out, bufs = refs[:count], refs[count], refs[count + 1 : 2 * count + 1]
+    in_sem, out_sem = refs[2 * count + 1 :]
     me = lax.axis_index("dp")
-    half = buf.shape[1]
+    half = out.shape[1] // (2 * n)
     loads = []
     for i, piece in enumerate(pieces):
-        copy = pltpu.make_async_copy(piece, buf.at[i], in_sem.at[i])
+        copy = pltpu.make_async_copy(piece, bufs[i], in_sem.at[i])
         copy.start()
         loads.append(copy)
     stores = []
-    for i, (layer, side, offset) in enumerate(spots):
+    for i, (start, side, offset) in enumerate(spots):
         loads[i].wait()
-        row = pl.multiple_of((2 * lax.rem(me + offset, n) + side) * half, 16)
-        copy = pltpu.make_async_copy(buf.at[i], out.at[layer, pl.ds(row, half)], out_sem.at[i])
+        row = pl.multiple_of((2 * lax.rem(me + offset, n) + side) * half + start, 16)
+        copy = pltpu.make_async_copy(bufs[i], out.at[:, pl.ds(row, bufs[i].shape[1])], out_sem.at[i])
         copy.start()
         stores.append(copy)
     for copy in stores:
@@ -240,14 +250,13 @@
 
 def place(n, shape, pieces):
     spots = tuple(pieces)
-    piece = pieces[spots[0]]
-    moved = 2 * len(spots) * piece.size * 2
+    moved = 4 * sum(piece.size for piece in pieces.values())
     return pl.pallas_call(
         functools.partial(place_kernel, n, spots),
         out_shape=jax.ShapeDtypeStruct(shape, BF16),
         in_specs=[pl.BlockSpec(memory_space=pl.ANY)] * len(spots),
         out_specs=pl.BlockSpec(memory_space=pl.ANY),
-        scratch_shapes=[pltpu.VMEM((len(spots), *piece.shape), BF16)] + [pltpu.SemaphoreType.DMA((len(spots),))] * 2,
+        scratch_shapes=[pltpu.VMEM(piece.shape, BF16) for piece in pieces.values()] + [pltpu.SemaphoreType.DMA((len(spots),))] * 2,
         cost_estimate=pl.CostEstimate(flops=moved, bytes_accessed=moved, transcendentals=0),
         name="place",
     )(*pieces.values())
@@ -287,23 +296,22 @@
 
 
 def gather(n, shape, own):
+    half = shape[1] // (2 * n)
     right, left = ([(i, (i + way) % n) for i in range(n)] for way in (1, n - 1))
     near, far = {}, {}
-    for layer, sides in enumerate(own):
+    for i, (start, _) in enumerate(cuts(half)):
         for side, ahead in enumerate((right, left)):
-            near[layer, side, 0] = sides[side]
-            near[layer, side, (n - 1, 1)[side]] = lax.ppermute(sides[side], "dp", ahead)
+            near[start, side, 0] = own[i][side]
+            near[start, side, (n - 1, 1)[side]] = lax.ppermute(own[i][side], "dp", ahead)
         for side, behind in enumerate((left, right)):
-            near[layer, side, (1, n - 1)[side]] = lax.ppermute(sides[side], "dp", behind)
-    for layer, sides in enumerate(own):
+            near[start, side, (1, n - 1)[side]] = lax.ppermute(own[i][side], "dp", behind)
+    for start, _ in cuts(half):
         for side, ahead in enumerate((right, left)):
-            far[layer, side] = lax.ppermute(near[layer, side, (n - 1, 1)[side]], "dp", ahead)
-    early = {(layer, side, 2): far[layer, side] for layer in range(len(own) - 1) for side in (0, 1)}
-    whole = place(n, shape, {**near, **early})
+            far[start, side] = lax.ppermute(near[start, side, (n - 1, 1)[side]], "dp", ahead)
+    whole = place(n, shape, near)
     opposite = lax.rem(lax.axis_index("dp") + 2, n)
-    for side in (0, 1):
-        piece = far[len(own) - 1, side]
-        whole = lax.dynamic_update_slice(whole, piece[None], (len(own) - 1, (2 * opposite + side) * piece.shape[0], 0))
+    for (start, side), piece in far.items():
+        whole = lax.dynamic_update_slice(whole, piece, (0, (2 * opposite + side) * half + start, 0))
     return whole
 
 
@@ -315,7 +323,6 @@
 
     def inner(*arrays):
         terms, weights, m, v = (arrays[i : i + 3] for i in (0, 3, 6, 9))
-        layers = m[0].shape[0]
         out = list(reduce_and_step(n, GATHERED, terms, weights, m, v))
         sums = [out.pop(0) for _ in range(3)]
         held, new, pairs = [], [], []
@@ -324,7 +331,7 @@
             if whole:
                 held.append(out.pop(0))
             else:
-                new.append(gather(n, weights[k].shape, [[out.pop(0) for _ in range(2)] for _ in range(layers)]))
+                new.append(gather(n, weights[k].shape, [[out.pop(0) for _ in range(2)] for _ in cuts(m[k].shape[1] // 2)]))
         new = [*carry(held), *new]
         return (*new, *(one[0] for one in pairs), *(one[1] for one in pairs))
 

time: 465 us -> 467 us (level)
  transfers between devices with their start and end apart: 12 -> 12, of which waited for: 4 -> 3; matrix products, arithmetic and copies ran while one was open for 5% -> 5% of each run, Pallas kernels for 4% -> 4%
where the time goes in v5:
time: 467 us
  Pallas kernels  397 us (85%)
  waiting for transfers between devices  23.7 us (5%)
  other arithmetic  20.9 us (4%)
  starting transfers between devices  18.9 us (4%)
  local copies, waits for them, and re-layouts  5.31 us (1%)
    pallas_call x1, Pallas kernels, reduce_and_step(): pl.pallas_call(functools.partial(kernel, n, layers, gathered), out_shape=...  379 us
    ppermute x4, waiting for transfers between devices, gather(): lax.ppermute(own[i][side], 'dp', ahead)  21.9 us
    add x2, other arithmetic, moments(): return (0.9 * m + 0.1 * g, 0.95 * v + 0.05 * g * g)  20.9 us
    pallas_call x1, Pallas kernels, carry(): pl.pallas_call(functools.partial(carry_kernel, parts), out_shape=[jax.Sha...  13.1 us
  transfers between devices with their start and end apart: 12, of which 3 were waited for; matrix products, arithmetic and copies ran while one was open for 5% of the time, Pallas kernels for 4%

profile of v5, /device:TPU:112, one launch (start us, length us, event | category | flops | bytes accessed | tf_op | source)
XLA Modules:
  0.0 466.6 jit_solution(4233429857746846748)
XLA Ops:
  0.6 378.5 %reduce_and_step.1 = (bf16[2,224,2560]{2,1,0:T(8,128)(2,1)}, bf16[2,224,2560]{2,1,0:T(8,128)(2,1)}, bf16[2,640,896]{2,1,0:T(8,128)(2,1)}, bf16[2,896,2560]{2,1,0...) custom-call(bf16[1,2,896,2560]{3,2,1,0:T(8,128)(2,1)} %refs_0_.1, ...), custom_call_target="tpu_custom_call" | custom-call | tf_op jit(solution)/shard_map/reduce_and_step/pallas_call | solution.py:216
  379.2 2.2 collective-permute-start
  381.4 1.1 collective-permute-start.1
  382.5 0.9 collective-permute-start.4
  383.4 2.3 collective-permute-start.5
  385.7 0.0 collective-permute-start.2
  385.7 18.8 %collective-permute-done.4.refs_7_ = bf16[2,64,896]{2,1,0:T(8,128)(2,1)S(1)} collective-permute-done((bf16[2,64,896]{2,1,0:T(8,128)(2,1)}, bf16[2,64,896]{2,1,0:T(8,128)(2,1)S(1)}, u32[]{:S(2)}, u32[]{:S(2)}) %collective-permute-start.4) | collective-permute-done | bytes 229408 | tf_op jit(solution)/shard_map/ppermute | solution.py:305
  404.6 0.0 copy-start.5
  404.6 2.2 collective-permute-start.3
  406.7 3.0 collective-permute-done.5.refs_9_
  409.7 0.0 copy-start.4
  409.7 2.3 collective-permute-start.6
  412.0 0.0 collective-permute-done.refs_1_
  412.0 0.0 collective-permute-start.8
  412.0 0.0 collective-permute-done.1.refs_3_
  412.0 0.0 copy-start.3
  412.1 3.2 collective-permute-start.9
  415.3 0.0 copy-done.5
  415.3 0.0 copy-start
  415.3 0.0 copy-start.1
  415.3 0.0 copy-start.2
  415.3 15.9 %fusion.3 = (f32[2,224,2560]{2,1,0:T(8,128)}, f32[2,224,2560]{2,1,0:T(8,128)}, f32[2,224,2560]{2,1,0:T(8,128)}, f32[2,224,2560]{2,1,0:T(8,128)}) fusion(bf16[2,224,2560]{2,1,0:T(8,128)(2,1)} %get-tuple-element.28, f32[2,224,2560]{2,1,0:T(8,128)} %refs_9_.1, f32[2,224,2560]{2,1,0:T(8,128)} %refs_6_.1, bf16[2,224,2560]{2,1,0:T(8,128)(2,1)} %get-tuple-element.29, ...), kind=kLoop, calls=%fused_computation.9 | loop fusion | flops 18350080 | bytes 41287680 | tf_op jit(solution)/shard_map/add | solution.py:21
  431.2 0.0 copy-done.3
  431.2 1.9 collective-permute-done.6.refs_10_
  433.1 1.3 collective-permute-start.7
  434.4 0.0 copy-done
  434.4 0.0 copy-done.1
  434.4 0.0 copy-done.2
  434.4 4.9 %fusion.5 = (f32[2,640,896]{2,1,0:T(8,128)}, f32[2,640,896]{2,1,0:T(8,128)}) fusion(bf16[2,640,896]{2,1,0:T(8,128)(2,1)S(1)} %copy-done.2, f32[2,640,896]{2,1,0:T(8,128)S(1)} %copy-done.1, f32[2,640,896]{2,1,0:T(8,128)S(1)} %copy-done), kind=kLoop, calls=%fused_computation.11 | loop fusion | flops 9175040 | bytes 20643840 | tf_op jit(solution)/shard_map/add | solution.py:21
  439.4 0.0 copy-start.6
  439.4 13.1 %carry.1 = (bf16[2,896,2560]{2,1,0:T(8,128)(2,1)}, bf16[2,896,2560]{2,1,0:T(8,128)(2,1)}) custom-call(bf16[2,896,2560]{2,1,0:T(8,128)(2,1)} %get-tuple-element.20.refs_0_, bf16[2,896,2560]{2,1,0:T(8,128)(2,1)} %get-tuple-element.21.refs_1_), custom_call_target="tpu_custom_call" | custom-call | flops 36700160 | bytes 36700160 | tf_op jit(solution)/shard_map/carry/pallas_call | solution.py:287
  452.5 0.0 collective-permute-done.7.refs_11_
  452.5 0.0 copy-done.6
  452.5 0.8 collective-permute-start.10
  453.3 0.0 collective-permute-done.2.refs_4_
  453.3 0.0 copy-done.4
  453.3 2.5 collective-permute-start.11
  455.8 0.0 collective-permute-done.3.refs_5_
  455.8 5.5 %place.1 = bf16[2,2560,896]{2,1,0:T(8,128)(2,1)} custom-call(bf16[2,256,896]{2,1,0:T(8,128)(2,1)} %get-tuple-element.24.refs_0_, bf16[2,256,896]{2,1,0:T(8,128)(2,1)} %collective-permute-done.refs_1_, bf16[2,256,896]{2,1,0:T(8,128)(2,1)} %get-tuple-element.25.refs_2_, bf16[2,256,896]{2,1,0:T(8,128)(2,1)} %copy-done.3, ...), custom_call_target="tpu_custom_call" | custom-call | flops 13762560 | bytes 13762560 | tf_op jit(solution)/shard_map/place/pallas_call | solution.py:254
  461.3 0.0 collective-permute-done.8
  461.3 1.0 constant_dynamic-update-slice_fusion.3
  462.3 0.0 collective-permute-done.9
  462.3 1.0 constant_dynamic-update-slice_fusion.2
  463.3 0.0 collective-permute-done.10
  463.3 1.6 constant_dynamic-update-slice_fusion.1
  465.0 0.0 collective-permute-done.11
  465.0 1.6 constant_dynamic-update-slice_fusion
Async XLA Ops:
  379.2 32.9 %collective-permute-start = (bf16[2,256,896]{2,1,0:T(8,128)(2,1)}, bf16[2,256,896]{2,1,0:T(8,128)(2,1)}, u32[]{:S(2)}, u32[]{:S(2)}) collective-permute-start(bf16[2,256,896]{2,1,0:T(8,128)(2,1)} %get-tuple-element.24.refs_0_), channel_id=1, source_target_pairs={{0,1},{1,2},{2,3},{3,0},{4,5},{5,6},{6,7},{7,4},{8,9},{9,10},{10,1... | collective-permute-start | bytes 2752520 | tf_op jit(solution)/shard_map/ppermute | solution.py:305
  381.4 30.7 %collective-permute-start.1 = (bf16[2,256,896]{2,1,0:T(8,128)(2,1)}, bf16[2,256,896]{2,1,0:T(8,128)(2,1)S(1)}, u32[]{:S(2)}, u32[]{:S(2)}) collective-permute-start(bf16[2,256,896]{2,1,0:T(8,128)(2,1)} %get-tuple-element.25.refs_2_), channel_id=1, source_target_pairs={{0,3},{1,0},{2,1},{3,2},{4,7},{5,4},{6,5},{7,6},{8,11},{9,8},{10,9... | collective-permute-start | bytes 2752520 | tf_op jit(solution)/shard_map/ppermute | solution.py:305
  382.5 22.1 %collective-permute-start.4 = (bf16[2,64,896]{2,1,0:T(8,128)(2,1)}, bf16[2,64,896]{2,1,0:T(8,128)(2,1)S(1)}, u32[]{:S(2)}, u32[]{:S(2)}) collective-permute-start(bf16[2,64,896]{2,1,0:T(8,128)(2,1)} %get-tuple-element.26.refs_6_), channel_id=1, source_target_pairs={{0,1},{1,2},{2,3},{3,0},{4,5},{5,6},{6,7},{7,4},{8,9},{9,10},{10,1... | collective-permute-start | bytes 688136 | tf_op jit(solution)/shard_map/ppermute | solution.py:305
  383.4 26.3 %collective-permute-start.5 = (bf16[2,64,896]{2,1,0:T(8,128)(2,1)}, bf16[2,64,896]{2,1,0:T(8,128)(2,1)S(1)}, u32[]{:S(2)}, u32[]{:S(2)}) collective-permute-start(bf16[2,64,896]{2,1,0:T(8,128)(2,1)} %get-tuple-element.27.refs_8_), channel_id=1, source_target_pairs={{0,3},{1,0},{2,1},{3,2},{4,7},{5,4},{6,5},{7,6},{8,11},{9,8},{10,9... | collective-permute-start | bytes 688136 | tf_op jit(solution)/shard_map/ppermute | solution.py:305
  385.7 67.6 %collective-permute-start.2 = (bf16[2,256,896]{2,1,0:T(8,128)(2,1)}, bf16[2,256,896]{2,1,0:T(8,128)(2,1)}, u32[]{:S(2)}, u32[]{:S(2)}) collective-permute-start(bf16[2,256,896]{2,1,0:T(8,128)(2,1)} %get-tuple-element.24.refs_0_), channel_id=1, source_target_pairs={{0,3},{1,0},{2,1},{3,2},{4,7},{5,4},{6,5},{7,6},{8,11},{9,8},{10,9... | collective-permute-start | bytes 2752520 | tf_op jit(solution)/shard_map/ppermute | solution.py:307
  404.6 10.7 %copy-start.5 = (bf16[2,64,896]{2,1,0:T(8,128)(2,1)}, bf16[2,64,896]{2,1,0:T(8,128)(2,1)S(1)}, u32[]{:S(2)}) copy-start(bf16[2,64,896]{2,1,0:T(8,128)(2,1)S(1)} %collective-permute-done.4.refs_7_) | copy-start | bytes 688132
  404.6 51.3 %collective-permute-start.3 = (bf16[2,256,896]{2,1,0:T(8,128)(2,1)}, bf16[2,256,896]{2,1,0:T(8,128)(2,1)}, u32[]{:S(2)}, u32[]{:S(2)}) collective-permute-start(bf16[2,256,896]{2,1,0:T(8,128)(2,1)} %get-tuple-element.25.refs_2_), channel_id=1, source_target_pairs={{0,1},{1,2},{2,3},{3,0},{4,5},{5,6},{6,7},{7,4},{8,9},{9,10},{10,1... | collective-permute-start | bytes 2752520 | tf_op jit(solution)/shard_map/ppermute | solution.py:307
  409.7 43.6 %copy-start.4 = (bf16[2,64,896]{2,1,0:T(8,128)(2,1)}, bf16[2,64,896]{2,1,0:T(8,128)(2,1)S(1)}, u32[]{:S(2)}) copy-start(bf16[2,64,896]{2,1,0:T(8,128)(2,1)S(1)} %collective-permute-done.5.refs_9_) | copy-start | bytes 688132
  409.7 23.4 %collective-permute-start.6 = (bf16[2,64,896]{2,1,0:T(8,128)(2,1)}, bf16[2,64,896]{2,1,0:T(8,128)(2,1)}, u32[]{:S(2)}, u32[]{:S(2)}) collective-permute-start(bf16[2,64,896]{2,1,0:T(8,128)(2,1)} %get-tuple-element.26.refs_6_), channel_id=1, source_target_pairs={{0,3},{1,0},{2,1},{3,2},{4,7},{5,4},{6,5},{7,6},{8,11},{9,8},{10,9... | collective-permute-start | bytes 688136 | tf_op jit(solution)/shard_map/ppermute | solution.py:307
  412.0 49.3 %collective-permute-start.8 = (bf16[2,256,896]{2,1,0:T(8,128)(2,1)}, bf16[2,256,896]{2,1,0:T(8,128)(2,1)S(1)}, u32[]{:S(2)}, u32[]{:S(2)}) collective-permute-start(bf16[2,256,896]{2,1,0:T(8,128)(2,1)} %collective-permute-done.refs_1_), channel_id=1, source_target_pairs={{0,1},{1,2},{2,3},{3,0},{4,5},{5,6},{6,7},{7,4},{8,9},{9,10},{10,1... | collective-permute-start | bytes 2752520 | tf_op jit(solution)/shard_map/ppermute | solution.py:310
  412.0 19.2 %copy-start.3 = (bf16[2,256,896]{2,1,0:T(8,128)(2,1)}, bf16[2,256,896]{2,1,0:T(8,128)(2,1)S(1)}, u32[]{:S(2)}) copy-start(bf16[2,256,896]{2,1,0:T(8,128)(2,1)S(1)} %collective-permute-done.1.refs_3_) | copy-start | bytes 2752516
  412.1 50.3 %collective-permute-start.9 = (bf16[2,256,896]{2,1,0:T(8,128)(2,1)S(1)}, bf16[2,256,896]{2,1,0:T(8,128)(2,1)S(1)}, u32[]{:S(2)}, u32[]{:S(2)}) collective-permute-start(bf16[2,256,896]{2,1,0:T(8,128)(2,1)S(1)} %collective-permute-done.1.refs_3_), channel_id=1, source_target_pairs={{0,3},{1,0},{2,1},{3,2},{4,7},{5,4},{6,5},{7,6},{8,11},{9,8},{10,9... | collective-permute-start | bytes 2752520 | tf_op jit(solution)/shard_map/ppermute | solution.py:310
  415.3 19.2 %copy-start = (f32[2,640,896]{2,1,0:T(8,128)S(1)}, f32[2,640,896]{2,1,0:T(8,128)}, u32[]{:S(2)}) copy-start(f32[2,640,896]{2,1,0:T(8,128)} %refs_8_.1) | copy-start | bytes 13762564
  415.3 19.2 %copy-start.1 = (f32[2,640,896]{2,1,0:T(8,128)S(1)}, f32[2,640,896]{2,1,0:T(8,128)}, u32[]{:S(2)}) copy-start(f32[2,640,896]{2,1,0:T(8,128)} %refs_11_.1) | copy-start | bytes 13762564
  415.3 19.2 %copy-start.2 = (bf16[2,640,896]{2,1,0:T(8,128)(2,1)S(1)}, bf16[2,640,896]{2,1,0:T(8,128)(2,1)}, u32[]{:S(2)}) copy-start(bf16[2,640,896]{2,1,0:T(8,128)(2,1)} %get-tuple-element.30) | copy-start | bytes 6881284
  433.1 19.4 %collective-permute-start.7 = (bf16[2,64,896]{2,1,0:T(8,128)(2,1)}, bf16[2,64,896]{2,1,0:T(8,128)(2,1)}, u32[]{:S(2)}, u32[]{:S(2)}) collective-permute-start(bf16[2,64,896]{2,1,0:T(8,128)(2,1)} %get-tuple-element.27.refs_8_), channel_id=1, source_target_pairs={{0,1},{1,2},{2,3},{3,0},{4,5},{5,6},{6,7},{7,4},{8,9},{9,10},{10,1... | collective-permute-start | bytes 688136 | tf_op jit(solution)/shard_map/ppermute | solution.py:307
  439.4 13.1 %copy-start.6 = (bf16[2,64,896]{2,1,0:T(8,128)(2,1)S(1)}, bf16[2,64,896]{2,1,0:T(8,128)(2,1)}, u32[]{:S(2)}) copy-start(bf16[2,64,896]{2,1,0:T(8,128)(2,1)} %copy-done.5) | copy-start | bytes 688132
  452.5 10.8 %collective-permute-start.10 = (bf16[2,64,896]{2,1,0:T(8,128)(2,1)S(1)}, bf16[2,64,896]{2,1,0:T(8,128)(2,1)}, u32[]{:S(2)}, u32[]{:S(2)}) collective-permute-start(bf16[2,64,896]{2,1,0:T(8,128)(2,1)S(1)} %copy-done.6), channel_id=1, source_target_pairs={{0,1},{1,2},{2,3},{3,0},{4,5},{5,6},{6,7},{7,4},{8,9},{9,10},{10,1... | collective-permute-start | bytes 688136 | tf_op jit(solution)/shard_map/ppermute | solution.py:310
  453.3 11.7 %collective-permute-start.11 = (bf16[2,64,896]{2,1,0:T(8,128)(2,1)S(1)}, bf16[2,64,896]{2,1,0:T(8,128)(2,1)}, u32[]{:S(2)}, u32[]{:S(2)}) collective-permute-start(bf16[2,64,896]{2,1,0:T(8,128)(2,1)S(1)} %collective-permute-done.5.refs_9_), channel_id=1, source_target_pairs={{0,3},{1,0},{2,1},{3,2},{4,7},{5,4},{6,5},{7,6},{8,11},{9,8},{10,9... | collective-permute-start | bytes 688136 | tf_op jit(solution)/shard_map/ppermute | solution.py:310

commit v6 on v5

--- a/solution.py
+++ b/solution.py
@@ -34,7 +34,7 @@
 
 def cuts(half):
     last = max(16, half // 5 // 16 * 16)
-    return (0, half - last), (half - last, last)
+    return (0, last, half - last), (half - last, 0, last)
 
 
 def tiled(shape, body):
@@ -163,8 +163,8 @@
                     sent["near", c, side, way] = send(x, place, sem["near_s"].at[c, side, way], sem["near_r"].at[c, side, way], peer)
                 pending.append(local(x, place, sem["w_out"].at[c, side, 0]).wait)
             else:
-                for i, (start, size) in enumerate(cuts(half)):
-                    pending.append(local(x.at[pl.ds(start, size)], w_out[k][i][side].at[l], sem["w_out"].at[c, side, i]).wait)
+                for i, (*starts, size) in enumerate(cuts(half)):
+                    pending.append(local(x.at[pl.ds(starts[side], size)], w_out[k][i][side].at[l], sem["w_out"].at[c, side, i]).wait)
             if c + 1 < len(chunks):
                 load_moments(c + 1, side)
 
@@ -209,7 +209,7 @@
         if whole:
             new.append(jax.ShapeDtypeStruct(w.shape, BF16))
         else:
-            new += [jax.ShapeDtypeStruct((layers, size, piece[3]), BF16) for _, size in cuts(piece[2]) for _ in range(2)]
+            new += [jax.ShapeDtypeStruct((layers, size, piece[3]), BF16) for *_, size in cuts(piece[2]) for _ in range(2)]
     out_shape = blocks + new
     sems = [pltpu.SemaphoreType.DMA((chunks, 2, 2) if name in BOTH_WAYS else (chunks, 2)) for name in SEMAPHORES[:-1]]
     sems.append(pltpu.SemaphoreType.REGULAR((2,)))
@@ -299,19 +299,24 @@
     half = shape[1] // (2 * n)
     right, left = ([(i, (i + way) % n) for i in range(n)] for way in (1, n - 1))
     near, far = {}, {}
-    for i, (start, _) in enumerate(cuts(half)):
+    for i, (*starts, _) in enumerate(cuts(half)):
         for side, ahead in enumerate((right, left)):
-            near[start, side, 0] = own[i][side]
-            near[start, side, (n - 1, 1)[side]] = lax.ppermute(own[i][side], "dp", ahead)
+            near[starts[side], side, 0] = own[i][side]
+            near[starts[side], side, (n - 1, 1)[side]] = lax.ppermute(own[i][side], "dp", ahead)
         for side, behind in enumerate((left, right)):
-            near[start, side, (1, n - 1)[side]] = lax.ppermute(own[i][side], "dp", behind)
-    for start, _ in cuts(half):
+            near[starts[side], side, (1, n - 1)[side]] = lax.ppermute(own[i][side], "dp", behind)
+    for i, (*starts, _) in enumerate(cuts(half)):
         for side, ahead in enumerate((right, left)):
-            far[start, side] = lax.ppermute(near[start, side, (n - 1, 1)[side]], "dp", ahead)
+            far[i, side] = lax.ppermute(near[starts[side], side, (n - 1, 1)[side]], "dp", ahead)
     whole = place(n, shape, near)
     opposite = lax.rem(lax.axis_index("dp") + 2, n)
-    for (start, side), piece in far.items():
-        whole = lax.dynamic_update_slice(whole, piece, (0, (2 * opposite + side) * half + start, 0))
+    for i, (*starts, _) in enumerate(cuts(half)):
+        row = 2 * opposite * half
+        if i == 0:
+            for side in (0, 1):
+                whole = lax.dynamic_update_slice(whole, far[i, side], (0, row + side * half + starts[side], 0))
+        else:
+            whole = lax.dynamic_update_slice(whole, jnp.concatenate([far[i, 0], far[i, 1]], 1), (0, row + starts[0], 0))
     return whole
 
 

time: 467 us -> 464 us (level)
  no operation moved by 1% of the time
where the time goes in v6:
time: 464 us
  Pallas kernels  397 us (86%)
  waiting for transfers between devices  23.7 us (5%)
  other arithmetic  22.7 us (5%)
  starting transfers between devices  17.7 us (4%)
    pallas_call x1, Pallas kernels, reduce_and_step(): pl.pallas_call(functools.partial(kernel, n, layers, gathered), out_shape=...  379 us
    ppermute x4, waiting for transfers between devices, gather(): lax.ppermute(own[i][side], 'dp', ahead)  21.9 us
    add x2, other arithmetic, moments(): return (0.9 * m + 0.1 * g, 0.95 * v + 0.05 * g * g)  20.9 us
    pallas_call x1, Pallas kernels, carry(): pl.pallas_call(functools.partial(carry_kernel, parts), out_shape=[jax.Sha...  13.1 us
  transfers between devices with their start and end apart: 12, of which 3 were waited for; matrix products, arithmetic and copies ran while one was open for 5% of the time, Pallas kernels for 4%

profile of v6, /device:TPU:112, one launch (start us, length us, event | category | flops | bytes accessed | tf_op | source)
XLA Modules:
  0.0 464.0 jit_solution(17560969935785976516)
XLA Ops:
  0.6 378.5 %reduce_and_step.1 = (bf16[2,224,2560]{2,1,0:T(8,128)(2,1)}, bf16[2,224,2560]{2,1,0:T(8,128)(2,1)}, bf16[2,640,896]{2,1,0:T(8,128)(2,1)}, bf16[2,896,2560]{2,1,0...) custom-call(bf16[1,2,896,2560]{3,2,1,0:T(8,128)(2,1)} %refs_0_.1, ...), custom_call_target="tpu_custom_call" | custom-call | tf_op jit(solution)/shard_map/reduce_and_step/pallas_call | solution.py:216
  379.2 2.2 collective-permute-start
  381.4 1.1 collective-permute-start.1
  382.5 0.9 collective-permute-start.4
  383.4 2.3 collective-permute-start.5
  385.7 0.0 collective-permute-start.2
  385.7 18.8 %collective-permute-done.4.refs_7_ = bf16[2,64,896]{2,1,0:T(8,128)(2,1)S(1)} collective-permute-done((bf16[2,64,896]{2,1,0:T(8,128)(2,1)}, bf16[2,64,896]{2,1,0:T(8,128)(2,1)S(1)}, u32[]{:S(2)}, u32[]{:S(2)}) %collective-permute-start.4) | collective-permute-done | bytes 229408 | tf_op jit(solution)/shard_map/ppermute | solution.py:305
  404.6 0.0 copy-start.4
  404.6 2.2 collective-permute-start.3
  406.7 3.0 collective-permute-done.5.refs_9_
  409.7 0.0 copy-start.5
  409.7 2.3 collective-permute-start.6
  412.0 0.0 collective-permute-done.refs_1_
  412.0 0.0 collective-permute-start.8
  412.0 0.0 collective-permute-done.1.refs_3_
  412.0 0.0 copy-start.3
  412.1 3.2 collective-permute-start.9
  415.3 0.0 copy-done.5
  415.3 0.0 copy-start
  415.3 0.0 copy-start.1
  415.3 0.0 copy-start.2
  415.3 15.9 %fusion.3 = (f32[2,224,2560]{2,1,0:T(8,128)}, f32[2,224,2560]{2,1,0:T(8,128)}, f32[2,224,2560]{2,1,0:T(8,128)}, f32[2,224,2560]{2,1,0:T(8,128)}) fusion(bf16[2,224,2560]{2,1,0:T(8,128)(2,1)} %get-tuple-element.28, f32[2,224,2560]{2,1,0:T(8,128)} %refs_9_.1, f32[2,224,2560]{2,1,0:T(8,128)} %refs_6_.1, bf16[2,224,2560]{2,1,0:T(8,128)(2,1)} %get-tuple-element.29, ...), kind=kLoop, calls=%fused_computation.9 | loop fusion | flops 18350080 | bytes 41287680 | tf_op jit(solution)/shard_map/add | solution.py:21
  431.2 0.0 copy-done.3
  431.2 1.9 collective-permute-done.6.refs_10_
  433.1 1.3 collective-permute-start.7
  434.4 0.0 copy-done
  434.4 0.0 copy-done.1
  434.4 0.0 copy-done.2
  434.4 4.9 %fusion.5 = (f32[2,640,896]{2,1,0:T(8,128)}, f32[2,640,896]{2,1,0:T(8,128)}) fusion(bf16[2,640,896]{2,1,0:T(8,128)(2,1)S(1)} %copy-done.2, f32[2,640,896]{2,1,0:T(8,128)S(1)} %copy-done.1, f32[2,640,896]{2,1,0:T(8,128)S(1)} %copy-done), kind=kLoop, calls=%fused_computation.11 | loop fusion | flops 9175040 | bytes 20643840 | tf_op jit(solution)/shard_map/add | solution.py:21
  439.4 0.0 copy-start.6
  439.4 13.1 %carry.1 = (bf16[2,896,2560]{2,1,0:T(8,128)(2,1)}, bf16[2,896,2560]{2,1,0:T(8,128)(2,1)}) custom-call(bf16[2,896,2560]{2,1,0:T(8,128)(2,1)} %get-tuple-element.20.refs_0_, bf16[2,896,2560]{2,1,0:T(8,128)(2,1)} %get-tuple-element.21.refs_1_), custom_call_target="tpu_custom_call" | custom-call | flops 36700160 | bytes 36700160 | tf_op jit(solution)/shard_map/carry/pallas_call | solution.py:287
  452.5 0.0 collective-permute-done.7.refs_11_
  452.5 0.0 copy-done.6
  452.5 2.0 collective-permute-start.11
  454.5 0.0 collective-permute-done.2.refs_4_
  454.5 0.0 copy-done.4
  454.5 0.1 collective-permute-start.10
  454.6 0.0 collective-permute-done.3.refs_5_
  454.6 5.5 %place.1 = bf16[2,2560,896]{2,1,0:T(8,128)(2,1)} custom-call(bf16[2,256,896]{2,1,0:T(8,128)(2,1)} %get-tuple-element.24.refs_0_, bf16[2,256,896]{2,1,0:T(8,128)(2,1)} %collective-permute-done.refs_1_, bf16[2,256,896]{2,1,0:T(8,128)(2,1)} %get-tuple-element.25.refs_2_, bf16[2,256,896]{2,1,0:T(8,128)(2,1)} %copy-done.3, ...), custom_call_target="tpu_custom_call" | custom-call | flops 13762560 | bytes 13762560 | tf_op jit(solution)/shard_map/place/pallas_call | solution.py:254
  460.1 0.0 collective-permute-done.8
  460.1 1.0 constant_dynamic-update-slice_fusion.1
  461.1 0.0 collective-permute-done.9
  461.1 1.0 constant_dynamic-update-slice_fusion
  462.1 0.0 collective-permute-done.11
  462.1 0.0 collective-permute-done.10
  462.1 1.9 maximum_dynamic-update-slice_fusion
Async XLA Ops:
  379.2 32.9 %collective-permute-start = (bf16[2,256,896]{2,1,0:T(8,128)(2,1)}, bf16[2,256,896]{2,1,0:T(8,128)(2,1)}, u32[]{:S(2)}, u32[]{:S(2)}) collective-permute-start(bf16[2,256,896]{2,1,0:T(8,128)(2,1)} %get-tuple-element.24.refs_0_), channel_id=1, source_target_pairs={{0,1},{1,2},{2,3},{3,0},{4,5},{5,6},{6,7},{7,4},{8,9},{9,10},{10,1... | collective-permute-start | bytes 2752520 | tf_op jit(solution)/shard_map/ppermute | solution.py:305
  381.4 30.7 %collective-permute-start.1 = (bf16[2,256,896]{2,1,0:T(8,128)(2,1)}, bf16[2,256,896]{2,1,0:T(8,128)(2,1)S(1)}, u32[]{:S(2)}, u32[]{:S(2)}) collective-permute-start(bf16[2,256,896]{2,1,0:T(8,128)(2,1)} %get-tuple-element.25.refs_2_), channel_id=1, source_target_pairs={{0,3},{1,0},{2,1},{3,2},{4,7},{5,4},{6,5},{7,6},{8,11},{9,8},{10,9... | collective-permute-start | bytes 2752520 | tf_op jit(solution)/shard_map/ppermute | solution.py:305
  382.5 22.1 %collective-permute-start.4 = (bf16[2,64,896]{2,1,0:T(8,128)(2,1)}, bf16[2,64,896]{2,1,0:T(8,128)(2,1)S(1)}, u32[]{:S(2)}, u32[]{:S(2)}) collective-permute-start(bf16[2,64,896]{2,1,0:T(8,128)(2,1)} %get-tuple-element.26.refs_6_), channel_id=1, source_target_pairs={{0,1},{1,2},{2,3},{3,0},{4,5},{5,6},{6,7},{7,4},{8,9},{9,10},{10,1... | collective-permute-start | bytes 688136 | tf_op jit(solution)/shard_map/ppermute | solution.py:305
  383.4 26.3 %collective-permute-start.5 = (bf16[2,64,896]{2,1,0:T(8,128)(2,1)}, bf16[2,64,896]{2,1,0:T(8,128)(2,1)S(1)}, u32[]{:S(2)}, u32[]{:S(2)}) collective-permute-start(bf16[2,64,896]{2,1,0:T(8,128)(2,1)} %get-tuple-element.27.refs_8_), channel_id=1, source_target_pairs={{0,3},{1,0},{2,1},{3,2},{4,7},{5,4},{6,5},{7,6},{8,11},{9,8},{10,9... | collective-permute-start | bytes 688136 | tf_op jit(solution)/shard_map/ppermute | solution.py:305
  385.7 68.8 %collective-permute-start.2 = (bf16[2,256,896]{2,1,0:T(8,128)(2,1)}, bf16[2,256,896]{2,1,0:T(8,128)(2,1)}, u32[]{:S(2)}, u32[]{:S(2)}) collective-permute-start(bf16[2,256,896]{2,1,0:T(8,128)(2,1)} %get-tuple-element.24.refs_0_), channel_id=1, source_target_pairs={{0,3},{1,0},{2,1},{3,2},{4,7},{5,4},{6,5},{7,6},{8,11},{9,8},{10,9... | collective-permute-start | bytes 2752520 | tf_op jit(solution)/shard_map/ppermute | solution.py:307
  404.6 49.9 %copy-start.4 = (bf16[2,64,896]{2,1,0:T(8,128)(2,1)}, bf16[2,64,896]{2,1,0:T(8,128)(2,1)S(1)}, u32[]{:S(2)}) copy-start(bf16[2,64,896]{2,1,0:T(8,128)(2,1)S(1)} %collective-permute-done.4.refs_7_) | copy-start | bytes 688132
  404.6 50.1 %collective-permute-start.3 = (bf16[2,256,896]{2,1,0:T(8,128)(2,1)}, bf16[2,256,896]{2,1,0:T(8,128)(2,1)}, u32[]{:S(2)}, u32[]{:S(2)}) collective-permute-start(bf16[2,256,896]{2,1,0:T(8,128)(2,1)} %get-tuple-element.25.refs_2_), channel_id=1, source_target_pairs={{0,1},{1,2},{2,3},{3,0},{4,5},{5,6},{6,7},{7,4},{8,9},{9,10},{10,1... | collective-permute-start | bytes 2752520 | tf_op jit(solution)/shard_map/ppermute | solution.py:307
  409.7 5.5 %copy-start.5 = (bf16[2,64,896]{2,1,0:T(8,128)(2,1)}, bf16[2,64,896]{2,1,0:T(8,128)(2,1)S(1)}, u32[]{:S(2)}) copy-start(bf16[2,64,896]{2,1,0:T(8,128)(2,1)S(1)} %collective-permute-done.5.refs_9_) | copy-start | bytes 688132
  409.7 23.4 %collective-permute-start.6 = (bf16[2,64,896]{2,1,0:T(8,128)(2,1)}, bf16[2,64,896]{2,1,0:T(8,128)(2,1)}, u32[]{:S(2)}, u32[]{:S(2)}) collective-permute-start(bf16[2,64,896]{2,1,0:T(8,128)(2,1)} %get-tuple-element.26.refs_6_), channel_id=1, source_target_pairs={{0,3},{1,0},{2,1},{3,2},{4,7},{5,4},{6,5},{7,6},{8,11},{9,8},{10,9... | collective-permute-start | bytes 688136 | tf_op jit(solution)/shard_map/ppermute | solution.py:307
  412.0 48.1 %collective-permute-start.8 = (bf16[2,256,896]{2,1,0:T(8,128)(2,1)}, bf16[2,256,896]{2,1,0:T(8,128)(2,1)S(1)}, u32[]{:S(2)}, u32[]{:S(2)}) collective-permute-start(bf16[2,256,896]{2,1,0:T(8,128)(2,1)} %collective-permute-done.refs_1_), channel_id=1, source_target_pairs={{0,1},{1,2},{2,3},{3,0},{4,5},{5,6},{6,7},{7,4},{8,9},{9,10},{10,1... | collective-permute-start | bytes 2752520 | tf_op jit(solution)/shard_map/ppermute | solution.py:310
  412.0 19.2 %copy-start.3 = (bf16[2,256,896]{2,1,0:T(8,128)(2,1)}, bf16[2,256,896]{2,1,0:T(8,128)(2,1)S(1)}, u32[]{:S(2)}) copy-start(bf16[2,256,896]{2,1,0:T(8,128)(2,1)S(1)} %collective-permute-done.1.refs_3_) | copy-start | bytes 2752516
  412.1 49.1 %collective-permute-start.9 = (bf16[2,256,896]{2,1,0:T(8,128)(2,1)S(1)}, bf16[2,256,896]{2,1,0:T(8,128)(2,1)S(1)}, u32[]{:S(2)}, u32[]{:S(2)}) collective-permute-start(bf16[2,256,896]{2,1,0:T(8,128)(2,1)S(1)} %collective-permute-done.1.refs_3_), channel_id=1, source_target_pairs={{0,3},{1,0},{2,1},{3,2},{4,7},{5,4},{6,5},{7,6},{8,11},{9,8},{10,9... | collective-permute-start | bytes 2752520 | tf_op jit(solution)/shard_map/ppermute | solution.py:310
  415.3 19.2 %copy-start = (f32[2,640,896]{2,1,0:T(8,128)S(1)}, f32[2,640,896]{2,1,0:T(8,128)}, u32[]{:S(2)}) copy-start(f32[2,640,896]{2,1,0:T(8,128)} %refs_8_.1) | copy-start | bytes 13762564
  415.3 19.2 %copy-start.1 = (f32[2,640,896]{2,1,0:T(8,128)S(1)}, f32[2,640,896]{2,1,0:T(8,128)}, u32[]{:S(2)}) copy-start(f32[2,640,896]{2,1,0:T(8,128)} %refs_11_.1) | copy-start | bytes 13762564
  415.3 19.2 %copy-start.2 = (bf16[2,640,896]{2,1,0:T(8,128)(2,1)S(1)}, bf16[2,640,896]{2,1,0:T(8,128)(2,1)}, u32[]{:S(2)}) copy-start(bf16[2,640,896]{2,1,0:T(8,128)(2,1)} %get-tuple-element.30) | copy-start | bytes 6881284
  433.1 19.4 %collective-permute-start.7 = (bf16[2,64,896]{2,1,0:T(8,128)(2,1)}, bf16[2,64,896]{2,1,0:T(8,128)(2,1)}, u32[]{:S(2)}, u32[]{:S(2)}) collective-permute-start(bf16[2,64,896]{2,1,0:T(8,128)(2,1)} %get-tuple-element.27.refs_8_), channel_id=1, source_target_pairs={{0,1},{1,2},{2,3},{3,0},{4,5},{5,6},{6,7},{7,4},{8,9},{9,10},{10,1... | collective-permute-start | bytes 688136 | tf_op jit(solution)/shard_map/ppermute | solution.py:307
  439.4 13.1 %copy-start.6 = (bf16[2,64,896]{2,1,0:T(8,128)(2,1)S(1)}, bf16[2,64,896]{2,1,0:T(8,128)(2,1)}, u32[]{:S(2)}) copy-start(bf16[2,64,896]{2,1,0:T(8,128)(2,1)} %copy-done.5) | copy-start | bytes 688132
  452.5 9.6 %collective-permute-start.11 = (bf16[2,64,896]{2,1,0:T(8,128)(2,1)S(1)}, bf16[2,64,896]{2,1,0:T(8,128)(2,1)}, u32[]{:S(2)}, u32[]{:S(2)}) collective-permute-start(bf16[2,64,896]{2,1,0:T(8,128)(2,1)S(1)} %copy-done.6), channel_id=1, source_target_pairs={{0,3},{1,0},{2,1},{3,2},{4,7},{5,4},{6,5},{7,6},{8,11},{9,8},{10,9... | collective-permute-start | bytes 688136 | tf_op jit(solution)/shard_map/ppermute | solution.py:310
  454.5 7.6 %collective-permute-start.10 = (bf16[2,64,896]{2,1,0:T(8,128)(2,1)S(1)}, bf16[2,64,896]{2,1,0:T(8,128)(2,1)}, u32[]{:S(2)}, u32[]{:S(2)}) collective-permute-start(bf16[2,64,896]{2,1,0:T(8,128)(2,1)S(1)} %collective-permute-done.4.refs_7_), channel_id=1, source_target_pairs={{0,1},{1,2},{2,3},{3,0},{4,5},{5,6},{6,7},{7,4},{8,9},{9,10},{10,1... | collective-permute-start | bytes 688136 | tf_op jit(solution)/shard_map/ppermute | solution.py:310

commit v7 on v6

--- a/solution.py
+++ b/solution.py
@@ -15,6 +15,7 @@
 BOTH_WAYS = ("near_s", "near_r", "w_out")
 SEMAPHORES = (*SENT, *LOCAL, *BOTH_WAYS, "again")
 LATER = 5
+POOLS = dict(far_s=3, dir_s=3, rel_s=3, fwd_s=2, near_s=2, term=3, own=4, w=4, m=1, v=1, g_out=2, w_out=2)
 
 
 def moments(m, v, g):
@@ -78,48 +79,62 @@
     lax.fori_loop(0, LATER * late, again, 0)
 
     chunks = [(k, layer) for k in range(count) for layer in range(layers)]
-    pending = []
+    busy = {}
+
+    def spot(name, c, *at):
+        key = (name, c % sem[name].shape[0], *at)
+        if key in busy:
+            busy.pop(key)()
+        return key, sem[name].at[key[1:]]
 
     def rows(k, block, side):
         half = far[k].shape[2]
         return pl.ds(pl.multiple_of((2 * block + side) * half, 16), half)
 
-    def send(src, dst, send_sem, recv_sem, peer):
+    def send(src, dst, name, c, at, peer):
+        key, send_sem = spot(name + "_s", c, *at)
+        recv_sem = sem[name + "_r"].at[(c, *at)]
         copy = pltpu.make_async_remote_copy(src, dst, send_sem, recv_sem, device_id={"dp": peer}, device_id_type=MESH)
         copy.start()
-        pending.append(copy.wait_send)
+        busy[key] = copy.wait_send
         return copy
 
-    def local(src, dst, s):
-        copy = pltpu.make_async_copy(src, dst, s)
+    def load(src, dst, name, c, side):
+        copy = pltpu.make_async_copy(src, dst, spot(name, c, side)[1])
         copy.start()
         return copy
 
+    def store(src, dst, name, c, *at):
+        key, done = spot(name, c, *at)
+        copy = pltpu.make_async_copy(src, dst, done)
+        copy.start()
+        busy[key] = copy.wait
+
     sent, loads, steps = {}, {}, {}
 
     def first(c):
         k, l = chunks[c]
         for side in (0, 1):
             sent["far", c, side] = send(
-                g[k].at[0, l, rows(k, opposite, side)], far[k].at[l, side], sem["far_s"].at[c, side], sem["far_r"].at[c, side], ahead[side]
+                g[k].at[0, l, rows(k, opposite, side)], far[k].at[l, side], "far", c, (side,), ahead[side]
             )
         for side in (0, 1):
             sent["dir", c, side] = send(
-                g[k].at[0, l, rows(k, behind[side], side)], direct[k].at[l, side], sem["dir_s"].at[c, side], sem["dir_r"].at[c, side], behind[side]
+                g[k].at[0, l, rows(k, behind[side], side)], direct[k].at[l, side], "dir", c, (side,), behind[side]
             )
         for side in (0, 1):
-            loads["term", c, side] = local(g[k].at[0, l, rows(k, ahead[side], side)], term[k].at[l, side], sem["term"].at[c, side])
-        for side in (0, 1):
-            loads["own", c, side] = local(g[k].at[0, l, rows(k, me, side)], own[k].at[l, side], sem["own"].at[c, side])
-            loads["w", c, side] = local(w[k].at[l, rows(k, me, side)], new[k].at[l, side], sem["w"].at[c, side])
+            loads["term", c, side] = load(g[k].at[0, l, rows(k, ahead[side], side)], term[k].at[l, side], "term", c, side)
+        for side in (0, 1):
+            loads["own", c, side] = load(g[k].at[0, l, rows(k, me, side)], own[k].at[l, side], "own", c, side)
+            loads["w", c, side] = load(w[k].at[l, rows(k, me, side)], new[k].at[l, side], "w", c, side)
 
     def load_moments(c, side):
         k, l = chunks[c]
         half = far[k].shape[2]
         here = pl.ds(side * half, half)
         steps[c, side] = (
-            local(m[k].at[l, here], m_buf[k].at[side], sem["m"].at[c, side]),
-            local(v[k].at[l, here], v_buf[k].at[side], sem["v"].at[c, side]),
+            load(m[k].at[l, here], m_buf[k].at[side], "m", c, side),
+            load(v[k].at[l, here], v_buf[k].at[side], "v", c, side),
         )
 
     def relay(c):
@@ -133,7 +148,7 @@
                 sums[r, cols] = (sums[r, cols].astype(F32) + mine[r, cols].astype(F32)).astype(BF16)
 
             tiled(sums.shape, add)
-            sent["rel", c, side] = send(sums, rel[k].at[l, side], sem["rel_s"].at[c, side], sem["rel_r"].at[c, side], ahead[side])
+            sent["rel", c, side] = send(sums, rel[k].at[l, side], "rel", c, (side,), ahead[side])
 
     def step(c):
         k, l = chunks[c]
@@ -143,8 +158,8 @@
             sent["rel", c, side].wait_recv()
             loads["own", c, side].wait()
             loads["w", c, side].wait()
-            for load in steps[c, side]:
-                load.wait()
+            for one in steps[c, side]:
+                one.wait()
             a, b, o, x = (array[k].at[l, side] for array in (rel, direct, own, new))
             ms, vs = m_buf[k].at[side], v_buf[k].at[side]
 
@@ -156,15 +171,15 @@
 
             tiled(o.shape, update)
             here = pl.ds(side * half, half)
-            pending.append(local(o, g_out[k].at[l, here], sem["g_out"].at[c, side]).wait)
+            store(o, g_out[k].at[l, here], "g_out", c, side)
             if gathered[k]:
                 place = w_out[k].at[l, rows(k, me, side)]
                 for way, peer in enumerate((ahead[side], behind[side])):
-                    sent["near", c, side, way] = send(x, place, sem["near_s"].at[c, side, way], sem["near_r"].at[c, side, way], peer)
-                pending.append(local(x, place, sem["w_out"].at[c, side, 0]).wait)
+                    sent["near", c, side, way] = send(x, place, "near", c, (side, way), peer)
+                store(x, place, "w_out", c, side, 0)
             else:
                 for i, (*starts, size) in enumerate(cuts(half)):
-                    pending.append(local(x.at[pl.ds(starts[side], size)], w_out[k][i][side].at[l], sem["w_out"].at[c, side, i]).wait)
+                    store(x.at[pl.ds(starts[side], size)], w_out[k][i][side].at[l], "w_out", c, side, i)
             if c + 1 < len(chunks):
                 load_moments(c + 1, side)
 
@@ -175,7 +190,7 @@
         for side in (0, 1):
             sent["near", c, side, 0].wait_recv()
             place = w_out[k].at[l, rows(k, behind[side], side)]
-            sent["fwd", c, side] = send(place, place, sem["fwd_s"].at[c, side], sem["fwd_r"].at[c, side], ahead[side])
+            sent["fwd", c, side] = send(place, place, "fwd", c, (side,), ahead[side])
 
     last = len(chunks)
     for c in range(min(2, last)):
@@ -194,7 +209,7 @@
     for key, copy in sent.items():
         if key[0] == "fwd" or (key[0] == "near" and key[3] == 1):
             copy.wait_recv()
-    for wait in pending:
+    for wait in busy.values():
         wait()
 
 
@@ -211,7 +226,9 @@
         else:
             new += [jax.ShapeDtypeStruct((layers, size, piece[3]), BF16) for *_, size in cuts(piece[2]) for _ in range(2)]
     out_shape = blocks + new
-    sems = [pltpu.SemaphoreType.DMA((chunks, 2, 2) if name in BOTH_WAYS else (chunks, 2)) for name in SEMAPHORES[:-1]]
+    whole_chunks = layers * max(k + 1 for k in range(count) if gathered[k])
+    depth = {name: POOLS.get(name, whole_chunks if name in ("near_r", "fwd_r") else chunks) for name in SEMAPHORES[:-1]}
+    sems = [pltpu.SemaphoreType.DMA((size, 2, 2) if name in BOTH_WAYS else (size, 2)) for name, size in depth.items()]
     sems.append(pltpu.SemaphoreType.REGULAR((2,)))
     return pl.pallas_call(
         functools.partial(kernel, n, layers, gathered),

time: 464 us -> 464 us (level)
  no operation moved by 1% of the time
where the time goes in v7:
time: 464 us
  Pallas kernels  397 us (86%)
  waiting for transfers between devices  23.7 us (5%)
  other arithmetic  22.7 us (5%)
  starting transfers between devices  17.7 us (4%)
    pallas_call x1, Pallas kernels, reduce_and_step(): pl.pallas_call(functools.partial(kernel, n, layers, gathered), out_shape=...  379 us
    ppermute x4, waiting for transfers between devices, gather(): lax.ppermute(own[i][side], 'dp', ahead)  21.9 us
    add x2, other arithmetic, moments(): return (0.9 * m + 0.1 * g, 0.95 * v + 0.05 * g * g)  20.9 us
    pallas_call x1, Pallas kernels, carry(): pl.pallas_call(functools.partial(carry_kernel, parts), out_shape=[jax.Sha...  13.1 us
  transfers between devices with their start and end apart: 12, of which 3 were waited for; matrix products, arithmetic and copies ran while one was open for 5% of the time, Pallas kernels for 4%

profile of v7, /device:TPU:112, one launch (start us, length us, event | category | flops | bytes accessed | tf_op | source)
XLA Modules:
  0.0 464.0 jit_solution(8653604375876024972)
XLA Ops:
  0.6 378.5 %reduce_and_step.1 = (bf16[2,224,2560]{2,1,0:T(8,128)(2,1)}, bf16[2,224,2560]{2,1,0:T(8,128)(2,1)}, bf16[2,640,896]{2,1,0:T(8,128)(2,1)}, bf16[2,896,2560]{2,1,0...) custom-call(bf16[1,2,896,2560]{3,2,1,0:T(8,128)(2,1)} %refs_0_.1, ...), custom_call_target="tpu_custom_call" | custom-call | tf_op jit(solution)/shard_map/reduce_and_step/pallas_call | solution.py:233
  379.2 2.2 collective-permute-start
  381.4 1.1 collective-permute-start.1
  382.5 0.9 collective-permute-start.4
  383.4 2.3 collective-permute-start.5
  385.7 0.0 collective-permute-start.2
  385.7 18.8 %collective-permute-done.4.refs_7_ = bf16[2,64,896]{2,1,0:T(8,128)(2,1)S(1)} collective-permute-done((bf16[2,64,896]{2,1,0:T(8,128)(2,1)}, bf16[2,64,896]{2,1,0:T(8,128)(2,1)S(1)}, u32[]{:S(2)}, u32[]{:S(2)}) %collective-permute-start.4) | collective-permute-done | bytes 229408 | tf_op jit(solution)/shard_map/ppermute | solution.py:322
  404.6 0.0 copy-start.4
  404.6 2.2 collective-permute-start.3
  406.7 3.0 collective-permute-done.5.refs_9_
  409.7 0.0 copy-start.5
  409.7 2.3 collective-permute-start.6
  412.0 0.0 collective-permute-done.refs_1_
  412.0 0.0 collective-permute-start.8
  412.0 0.0 collective-permute-done.1.refs_3_
  412.0 0.0 copy-start.3
  412.1 3.2 collective-permute-start.9
  415.3 0.0 copy-done.5
  415.3 0.0 copy-start
  415.3 0.0 copy-start.1
  415.3 0.0 copy-start.2
  415.3 15.9 %fusion.3 = (f32[2,224,2560]{2,1,0:T(8,128)}, f32[2,224,2560]{2,1,0:T(8,128)}, f32[2,224,2560]{2,1,0:T(8,128)}, f32[2,224,2560]{2,1,0:T(8,128)}) fusion(bf16[2,224,2560]{2,1,0:T(8,128)(2,1)} %get-tuple-element.28, f32[2,224,2560]{2,1,0:T(8,128)} %refs_9_.1, f32[2,224,2560]{2,1,0:T(8,128)} %refs_6_.1, bf16[2,224,2560]{2,1,0:T(8,128)(2,1)} %get-tuple-element.29, ...), kind=kLoop, calls=%fused_computation.9 | loop fusion | flops 18350080 | bytes 41287680 | tf_op jit(solution)/shard_map/add | solution.py:22
  431.2 0.0 copy-done.3
  431.2 1.9 collective-permute-done.6.refs_10_
  433.1 1.3 collective-permute-start.7
  434.4 0.0 copy-done
  434.4 0.0 copy-done.1
  434.4 0.0 copy-done.2
  434.4 4.9 %fusion.5 = (f32[2,640,896]{2,1,0:T(8,128)}, f32[2,640,896]{2,1,0:T(8,128)}) fusion(bf16[2,640,896]{2,1,0:T(8,128)(2,1)S(1)} %copy-done.2, f32[2,640,896]{2,1,0:T(8,128)S(1)} %copy-done.1, f32[2,640,896]{2,1,0:T(8,128)S(1)} %copy-done), kind=kLoop, calls=%fused_computation.11 | loop fusion | flops 9175040 | bytes 20643840 | tf_op jit(solution)/shard_map/add | solution.py:22
  439.4 0.0 copy-start.6
  439.4 13.1 %carry.1 = (bf16[2,896,2560]{2,1,0:T(8,128)(2,1)}, bf16[2,896,2560]{2,1,0:T(8,128)(2,1)}) custom-call(bf16[2,896,2560]{2,1,0:T(8,128)(2,1)} %get-tuple-element.20.refs_0_, bf16[2,896,2560]{2,1,0:T(8,128)(2,1)} %get-tuple-element.21.refs_1_), custom_call_target="tpu_custom_call" | custom-call | flops 36700160 | bytes 36700160 | tf_op jit(solution)/shard_map/carry/pallas_call | solution.py:304
  452.5 0.0 collective-permute-done.7.refs_11_
  452.5 0.0 copy-done.6
  452.5 2.0 collective-permute-start.11
  454.5 0.0 collective-permute-done.2.refs_4_
  454.5 0.0 copy-done.4
  454.5 0.1 collective-permute-start.10
  454.6 0.0 collective-permute-done.3.refs_5_
  454.6 5.5 %place.1 = bf16[2,2560,896]{2,1,0:T(8,128)(2,1)} custom-call(bf16[2,256,896]{2,1,0:T(8,128)(2,1)} %get-tuple-element.24.refs_0_, bf16[2,256,896]{2,1,0:T(8,128)(2,1)} %collective-permute-done.refs_1_, bf16[2,256,896]{2,1,0:T(8,128)(2,1)} %get-tuple-element.25.refs_2_, bf16[2,256,896]{2,1,0:T(8,128)(2,1)} %copy-done.3, ...), custom_call_target="tpu_custom_call" | custom-call | flops 13762560 | bytes 13762560 | tf_op jit(solution)/shard_map/place/pallas_call | solution.py:271
  460.1 0.0 collective-permute-done.8
  460.1 1.0 constant_dynamic-update-slice_fusion.1
  461.1 0.0 collective-permute-done.9
  461.1 1.0 constant_dynamic-update-slice_fusion
  462.1 0.0 collective-permute-done.11
  462.1 0.0 collective-permute-done.10
  462.1 1.9 maximum_dynamic-update-slice_fusion
Async XLA Ops:
  379.2 32.9 %collective-permute-start = (bf16[2,256,896]{2,1,0:T(8,128)(2,1)}, bf16[2,256,896]{2,1,0:T(8,128)(2,1)}, u32[]{:S(2)}, u32[]{:S(2)}) collective-permute-start(bf16[2,256,896]{2,1,0:T(8,128)(2,1)} %get-tuple-element.24.refs_0_), channel_id=1, source_target_pairs={{0,1},{1,2},{2,3},{3,0},{4,5},{5,6},{6,7},{7,4},{8,9},{9,10},{10,1... | collective-permute-start | bytes 2752520 | tf_op jit(solution)/shard_map/ppermute | solution.py:322
  381.4 30.7 %collective-permute-start.1 = (bf16[2,256,896]{2,1,0:T(8,128)(2,1)}, bf16[2,256,896]{2,1,0:T(8,128)(2,1)S(1)}, u32[]{:S(2)}, u32[]{:S(2)}) collective-permute-start(bf16[2,256,896]{2,1,0:T(8,128)(2,1)} %get-tuple-element.25.refs_2_), channel_id=1, source_target_pairs={{0,3},{1,0},{2,1},{3,2},{4,7},{5,4},{6,5},{7,6},{8,11},{9,8},{10,9... | collective-permute-start | bytes 2752520 | tf_op jit(solution)/shard_map/ppermute | solution.py:322
  382.5 22.1 %collective-permute-start.4 = (bf16[2,64,896]{2,1,0:T(8,128)(2,1)}, bf16[2,64,896]{2,1,0:T(8,128)(2,1)S(1)}, u32[]{:S(2)}, u32[]{:S(2)}) collective-permute-start(bf16[2,64,896]{2,1,0:T(8,128)(2,1)} %get-tuple-element.26.refs_6_), channel_id=1, source_target_pairs={{0,1},{1,2},{2,3},{3,0},{4,5},{5,6},{6,7},{7,4},{8,9},{9,10},{10,1... | collective-permute-start | bytes 688136 | tf_op jit(solution)/shard_map/ppermute | solution.py:322
  383.4 26.3 %collective-permute-start.5 = (bf16[2,64,896]{2,1,0:T(8,128)(2,1)}, bf16[2,64,896]{2,1,0:T(8,128)(2,1)S(1)}, u32[]{:S(2)}, u32[]{:S(2)}) collective-permute-start(bf16[2,64,896]{2,1,0:T(8,128)(2,1)} %get-tuple-element.27.refs_8_), channel_id=1, source_target_pairs={{0,3},{1,0},{2,1},{3,2},{4,7},{5,4},{6,5},{7,6},{8,11},{9,8},{10,9... | collective-permute-start | bytes 688136 | tf_op jit(solution)/shard_map/ppermute | solution.py:322
  385.7 68.8 %collective-permute-start.2 = (bf16[2,256,896]{2,1,0:T(8,128)(2,1)}, bf16[2,256,896]{2,1,0:T(8,128)(2,1)}, u32[]{:S(2)}, u32[]{:S(2)}) collective-permute-start(bf16[2,256,896]{2,1,0:T(8,128)(2,1)} %get-tuple-element.24.refs_0_), channel_id=1, source_target_pairs={{0,3},{1,0},{2,1},{3,2},{4,7},{5,4},{6,5},{7,6},{8,11},{9,8},{10,9... | collective-permute-start | bytes 2752520 | tf_op jit(solution)/shard_map/ppermute | solution.py:324
  404.6 49.9 %copy-start.4 = (bf16[2,64,896]{2,1,0:T(8,128)(2,1)}, bf16[2,64,896]{2,1,0:T(8,128)(2,1)S(1)}, u32[]{:S(2)}) copy-start(bf16[2,64,896]{2,1,0:T(8,128)(2,1)S(1)} %collective-permute-done.4.refs_7_) | copy-start | bytes 688132
  404.6 50.1 %collective-permute-start.3 = (bf16[2,256,896]{2,1,0:T(8,128)(2,1)}, bf16[2,256,896]{2,1,0:T(8,128)(2,1)}, u32[]{:S(2)}, u32[]{:S(2)}) collective-permute-start(bf16[2,256,896]{2,1,0:T(8,128)(2,1)} %get-tuple-element.25.refs_2_), channel_id=1, source_target_pairs={{0,1},{1,2},{2,3},{3,0},{4,5},{5,6},{6,7},{7,4},{8,9},{9,10},{10,1... | collective-permute-start | bytes 2752520 | tf_op jit(solution)/shard_map/ppermute | solution.py:324
  409.7 5.5 %copy-start.5 = (bf16[2,64,896]{2,1,0:T(8,128)(2,1)}, bf16[2,64,896]{2,1,0:T(8,128)(2,1)S(1)}, u32[]{:S(2)}) copy-start(bf16[2,64,896]{2,1,0:T(8,128)(2,1)S(1)} %collective-permute-done.5.refs_9_) | copy-start | bytes 688132
  409.7 23.4 %collective-permute-start.6 = (bf16[2,64,896]{2,1,0:T(8,128)(2,1)}, bf16[2,64,896]{2,1,0:T(8,128)(2,1)}, u32[]{:S(2)}, u32[]{:S(2)}) collective-permute-start(bf16[2,64,896]{2,1,0:T(8,128)(2,1)} %get-tuple-element.26.refs_6_), channel_id=1, source_target_pairs={{0,3},{1,0},{2,1},{3,2},{4,7},{5,4},{6,5},{7,6},{8,11},{9,8},{10,9... | collective-permute-start | bytes 688136 | tf_op jit(solution)/shard_map/ppermute | solution.py:324
  412.0 48.1 %collective-permute-start.8 = (bf16[2,256,896]{2,1,0:T(8,128)(2,1)}, bf16[2,256,896]{2,1,0:T(8,128)(2,1)S(1)}, u32[]{:S(2)}, u32[]{:S(2)}) collective-permute-start(bf16[2,256,896]{2,1,0:T(8,128)(2,1)} %collective-permute-done.refs_1_), channel_id=1, source_target_pairs={{0,1},{1,2},{2,3},{3,0},{4,5},{5,6},{6,7},{7,4},{8,9},{9,10},{10,1... | collective-permute-start | bytes 2752520 | tf_op jit(solution)/shard_map/ppermute | solution.py:327
  412.0 19.2 %copy-start.3 = (bf16[2,256,896]{2,1,0:T(8,128)(2,1)}, bf16[2,256,896]{2,1,0:T(8,128)(2,1)S(1)}, u32[]{:S(2)}) copy-start(bf16[2,256,896]{2,1,0:T(8,128)(2,1)S(1)} %collective-permute-done.1.refs_3_) | copy-start | bytes 2752516
  412.1 49.1 %collective-permute-start.9 = (bf16[2,256,896]{2,1,0:T(8,128)(2,1)S(1)}, bf16[2,256,896]{2,1,0:T(8,128)(2,1)S(1)}, u32[]{:S(2)}, u32[]{:S(2)}) collective-permute-start(bf16[2,256,896]{2,1,0:T(8,128)(2,1)S(1)} %collective-permute-done.1.refs_3_), channel_id=1, source_target_pairs={{0,3},{1,0},{2,1},{3,2},{4,7},{5,4},{6,5},{7,6},{8,11},{9,8},{10,9... | collective-permute-start | bytes 2752520 | tf_op jit(solution)/shard_map/ppermute | solution.py:327
  415.3 19.2 %copy-start = (f32[2,640,896]{2,1,0:T(8,128)S(1)}, f32[2,640,896]{2,1,0:T(8,128)}, u32[]{:S(2)}) copy-start(f32[2,640,896]{2,1,0:T(8,128)} %refs_8_.1) | copy-start | bytes 13762564
  415.3 19.2 %copy-start.1 = (f32[2,640,896]{2,1,0:T(8,128)S(1)}, f32[2,640,896]{2,1,0:T(8,128)}, u32[]{:S(2)}) copy-start(f32[2,640,896]{2,1,0:T(8,128)} %refs_11_.1) | copy-start | bytes 13762564
  415.3 19.2 %copy-start.2 = (bf16[2,640,896]{2,1,0:T(8,128)(2,1)S(1)}, bf16[2,640,896]{2,1,0:T(8,128)(2,1)}, u32[]{:S(2)}) copy-start(bf16[2,640,896]{2,1,0:T(8,128)(2,1)} %get-tuple-element.30) | copy-start | bytes 6881284
  433.1 19.4 %collective-permute-start.7 = (bf16[2,64,896]{2,1,0:T(8,128)(2,1)}, bf16[2,64,896]{2,1,0:T(8,128)(2,1)}, u32[]{:S(2)}, u32[]{:S(2)}) collective-permute-start(bf16[2,64,896]{2,1,0:T(8,128)(2,1)} %get-tuple-element.27.refs_8_), channel_id=1, source_target_pairs={{0,1},{1,2},{2,3},{3,0},{4,5},{5,6},{6,7},{7,4},{8,9},{9,10},{10,1... | collective-permute-start | bytes 688136 | tf_op jit(solution)/shard_map/ppermute | solution.py:324
  439.4 13.1 %copy-start.6 = (bf16[2,64,896]{2,1,0:T(8,128)(2,1)S(1)}, bf16[2,64,896]{2,1,0:T(8,128)(2,1)}, u32[]{:S(2)}) copy-start(bf16[2,64,896]{2,1,0:T(8,128)(2,1)} %copy-done.5) | copy-start | bytes 688132
  452.5 9.6 %collective-permute-start.11 = (bf16[2,64,896]{2,1,0:T(8,128)(2,1)S(1)}, bf16[2,64,896]{2,1,0:T(8,128)(2,1)}, u32[]{:S(2)}, u32[]{:S(2)}) collective-permute-start(bf16[2,64,896]{2,1,0:T(8,128)(2,1)S(1)} %copy-done.6), channel_id=1, source_target_pairs={{0,3},{1,0},{2,1},{3,2},{4,7},{5,4},{6,5},{7,6},{8,11},{9,8},{10,9... | collective-permute-start | bytes 688136 | tf_op jit(solution)/shard_map/ppermute | solution.py:327
  454.5 7.6 %collective-permute-start.10 = (bf16[2,64,896]{2,1,0:T(8,128)(2,1)S(1)}, bf16[2,64,896]{2,1,0:T(8,128)(2,1)}, u32[]{:S(2)}, u32[]{:S(2)}) collective-permute-start(bf16[2,64,896]{2,1,0:T(8,128)(2,1)S(1)} %collective-permute-done.4.refs_7_), channel_id=1, source_target_pairs={{0,1},{1,2},{2,3},{3,0},{4,5},{5,6},{6,7},{7,4},{8,9},{9,10},{10,1... | collective-permute-start | bytes 688136 | tf_op jit(solution)/shard_map/ppermute | solution.py:327

commit v8 on v7

--- a/solution.py
+++ b/solution.py
@@ -114,17 +114,17 @@
 
     def first(c):
         k, l = chunks[c]
-        for side in (0, 1):
+        for side in (1, 0):
             sent["far", c, side] = send(
                 g[k].at[0, l, rows(k, opposite, side)], far[k].at[l, side], "far", c, (side,), ahead[side]
             )
-        for side in (0, 1):
+        for side in (1, 0):
             sent["dir", c, side] = send(
                 g[k].at[0, l, rows(k, behind[side], side)], direct[k].at[l, side], "dir", c, (side,), behind[side]
             )
-        for side in (0, 1):
+        for side in (1, 0):
             loads["term", c, side] = load(g[k].at[0, l, rows(k, ahead[side], side)], term[k].at[l, side], "term", c, side)
-        for side in (0, 1):
+        for side in (1, 0):
             loads["own", c, side] = load(g[k].at[0, l, rows(k, me, side)], own[k].at[l, side], "own", c, side)
             loads["w", c, side] = load(w[k].at[l, rows(k, me, side)], new[k].at[l, side], "w", c, side)
 
@@ -139,7 +139,7 @@
 
     def relay(c):
         k, l = chunks[c]
-        for side in (0, 1):
+        for side in (1, 0):
             sent["far", c, side].wait_recv()
             loads["term", c, side].wait()
             sums, mine = far[k].at[l, side], term[k].at[l, side]
@@ -153,7 +153,7 @@
     def step(c):
         k, l = chunks[c]
         half = far[k].shape[2]
-        for side in (0, 1):
+        for side in (1, 0):
             sent["dir", c, side].wait_recv()
             sent["rel", c, side].wait_recv()
             loads["own", c, side].wait()

time: 464 us -> 464 us (level)
  no operation moved by 1% of the time
where the time goes in v8:
time: 464 us
  Pallas kernels  397 us (86%)
  waiting for transfers between devices  23.7 us (5%)
  other arithmetic  22.7 us (5%)
  starting transfers between devices  17.7 us (4%)
    pallas_call x1, Pallas kernels, reduce_and_step(): pl.pallas_call(functools.partial(kernel, n, layers, gathered), out_shape=...  379 us
    ppermute x4, waiting for transfers between devices, gather(): lax.ppermute(own[i][side], 'dp', ahead)  21.8 us
    add x2, other arithmetic, moments(): return (0.9 * m + 0.1 * g, 0.95 * v + 0.05 * g * g)  20.9 us
    pallas_call x1, Pallas kernels, carry(): pl.pallas_call(functools.partial(carry_kernel, parts), out_shape=[jax.Sha...  13.1 us
  transfers between devices with their start and end apart: 12, of which 3 were waited for; matrix products, arithmetic and copies ran while one was open for 5% of the time, Pallas kernels for 4%

profile of v8, /device:TPU:112, one launch (start us, length us, event | category | flops | bytes accessed | tf_op | source)
XLA Modules:
  0.0 464.0 jit_solution(18427608366543994079)
XLA Ops:
  0.6 378.5 %reduce_and_step.1 = (bf16[2,224,2560]{2,1,0:T(8,128)(2,1)}, bf16[2,224,2560]{2,1,0:T(8,128)(2,1)}, bf16[2,640,896]{2,1,0:T(8,128)(2,1)}, bf16[2,896,2560]{2,1,0...) custom-call(bf16[1,2,896,2560]{3,2,1,0:T(8,128)(2,1)} %refs_0_.1, ...), custom_call_target="tpu_custom_call" | custom-call | tf_op jit(solution)/shard_map/reduce_and_step/pallas_call | solution.py:233
  379.2 2.2 collective-permute-start
  381.4 1.1 collective-permute-start.1
  382.5 0.9 collective-permute-start.4
  383.4 2.3 collective-permute-start.5
  385.7 0.0 collective-permute-start.2
  385.7 18.8 %collective-permute-done.4.refs_7_ = bf16[2,64,896]{2,1,0:T(8,128)(2,1)S(1)} collective-permute-done((bf16[2,64,896]{2,1,0:T(8,128)(2,1)}, bf16[2,64,896]{2,1,0:T(8,128)(2,1)S(1)}, u32[]{:S(2)}, u32[]{:S(2)}) %collective-permute-start.4) | collective-permute-done | bytes 229408 | tf_op jit(solution)/shard_map/ppermute | solution.py:322
  404.6 0.0 copy-start.4
  404.6 2.2 collective-permute-start.3
  406.7 3.0 collective-permute-done.5.refs_9_
  409.7 0.0 copy-start.5
  409.7 2.3 collective-permute-start.6
  412.0 0.0 collective-permute-done.refs_1_
  412.0 0.0 collective-permute-start.8
  412.0 0.0 collective-permute-done.1.refs_3_
  412.0 0.0 copy-start.3
  412.1 3.2 collective-permute-start.9
  415.3 0.0 copy-done.5
  415.3 0.0 copy-start
  415.3 0.0 copy-start.1
  415.3 0.0 copy-start.2
  415.3 15.9 %fusion.3 = (f32[2,224,2560]{2,1,0:T(8,128)}, f32[2,224,2560]{2,1,0:T(8,128)}, f32[2,224,2560]{2,1,0:T(8,128)}, f32[2,224,2560]{2,1,0:T(8,128)}) fusion(bf16[2,224,2560]{2,1,0:T(8,128)(2,1)} %get-tuple-element.28, f32[2,224,2560]{2,1,0:T(8,128)} %refs_9_.1, f32[2,224,2560]{2,1,0:T(8,128)} %refs_6_.1, bf16[2,224,2560]{2,1,0:T(8,128)(2,1)} %get-tuple-element.29, ...), kind=kLoop, calls=%fused_computation.9 | loop fusion | flops 18350080 | bytes 41287680 | tf_op jit(solution)/shard_map/add | solution.py:22
  431.2 0.0 copy-done.3
  431.2 1.9 collective-permute-done.6.refs_10_
  433.1 1.3 collective-permute-start.7
  434.4 0.0 copy-done
  434.4 0.0 copy-done.1
  434.4 0.0 copy-done.2
  434.4 4.9 %fusion.5 = (f32[2,640,896]{2,1,0:T(8,128)}, f32[2,640,896]{2,1,0:T(8,128)}) fusion(bf16[2,640,896]{2,1,0:T(8,128)(2,1)S(1)} %copy-done.2, f32[2,640,896]{2,1,0:T(8,128)S(1)} %copy-done.1, f32[2,640,896]{2,1,0:T(8,128)S(1)} %copy-done), kind=kLoop, calls=%fused_computation.11 | loop fusion | flops 9175040 | bytes 20643840 | tf_op jit(solution)/shard_map/add | solution.py:22
  439.4 0.0 copy-start.6
  439.4 13.1 %carry.1 = (bf16[2,896,2560]{2,1,0:T(8,128)(2,1)}, bf16[2,896,2560]{2,1,0:T(8,128)(2,1)}) custom-call(bf16[2,896,2560]{2,1,0:T(8,128)(2,1)} %get-tuple-element.20.refs_0_, bf16[2,896,2560]{2,1,0:T(8,128)(2,1)} %get-tuple-element.21.refs_1_), custom_call_target="tpu_custom_call" | custom-call | flops 36700160 | bytes 36700160 | tf_op jit(solution)/shard_map/carry/pallas_call | solution.py:304
  452.5 0.0 collective-permute-done.7.refs_11_
  452.5 0.0 copy-done.6
  452.5 2.0 collective-permute-start.11
  454.5 0.0 collective-permute-done.2.refs_4_
  454.5 0.0 copy-done.4
  454.5 0.1 collective-permute-start.10
  454.6 0.0 collective-permute-done.3.refs_5_
  454.6 5.5 %place.1 = bf16[2,2560,896]{2,1,0:T(8,128)(2,1)} custom-call(bf16[2,256,896]{2,1,0:T(8,128)(2,1)} %get-tuple-element.24.refs_0_, bf16[2,256,896]{2,1,0:T(8,128)(2,1)} %collective-permute-done.refs_1_, bf16[2,256,896]{2,1,0:T(8,128)(2,1)} %get-tuple-element.25.refs_2_, bf16[2,256,896]{2,1,0:T(8,128)(2,1)} %copy-done.3, ...), custom_call_target="tpu_custom_call" | custom-call | flops 13762560 | bytes 13762560 | tf_op jit(solution)/shard_map/place/pallas_call | solution.py:271
  460.1 0.0 collective-permute-done.8
  460.1 1.0 constant_dynamic-update-slice_fusion.1
  461.1 0.0 collective-permute-done.9
  461.1 1.0 constant_dynamic-update-slice_fusion
  462.1 0.0 collective-permute-done.11
  462.1 0.0 collective-permute-done.10
  462.1 1.9 maximum_dynamic-update-slice_fusion
Async XLA Ops:
  379.2 32.9 %collective-permute-start = (bf16[2,256,896]{2,1,0:T(8,128)(2,1)}, bf16[2,256,896]{2,1,0:T(8,128)(2,1)}, u32[]{:S(2)}, u32[]{:S(2)}) collective-permute-start(bf16[2,256,896]{2,1,0:T(8,128)(2,1)} %get-tuple-element.24.refs_0_), channel_id=1, source_target_pairs={{0,1},{1,2},{2,3},{3,0},{4,5},{5,6},{6,7},{7,4},{8,9},{9,10},{10,1... | collective-permute-start | bytes 2752520 | tf_op jit(solution)/shard_map/ppermute | solution.py:322
  381.4 30.7 %collective-permute-start.1 = (bf16[2,256,896]{2,1,0:T(8,128)(2,1)}, bf16[2,256,896]{2,1,0:T(8,128)(2,1)S(1)}, u32[]{:S(2)}, u32[]{:S(2)}) collective-permute-start(bf16[2,256,896]{2,1,0:T(8,128)(2,1)} %get-tuple-element.25.refs_2_), channel_id=1, source_target_pairs={{0,3},{1,0},{2,1},{3,2},{4,7},{5,4},{6,5},{7,6},{8,11},{9,8},{10,9... | collective-permute-start | bytes 2752520 | tf_op jit(solution)/shard_map/ppermute | solution.py:322
  382.5 22.1 %collective-permute-start.4 = (bf16[2,64,896]{2,1,0:T(8,128)(2,1)}, bf16[2,64,896]{2,1,0:T(8,128)(2,1)S(1)}, u32[]{:S(2)}, u32[]{:S(2)}) collective-permute-start(bf16[2,64,896]{2,1,0:T(8,128)(2,1)} %get-tuple-element.26.refs_6_), channel_id=1, source_target_pairs={{0,1},{1,2},{2,3},{3,0},{4,5},{5,6},{6,7},{7,4},{8,9},{9,10},{10,1... | collective-permute-start | bytes 688136 | tf_op jit(solution)/shard_map/ppermute | solution.py:322
  383.4 26.3 %collective-permute-start.5 = (bf16[2,64,896]{2,1,0:T(8,128)(2,1)}, bf16[2,64,896]{2,1,0:T(8,128)(2,1)S(1)}, u32[]{:S(2)}, u32[]{:S(2)}) collective-permute-start(bf16[2,64,896]{2,1,0:T(8,128)(2,1)} %get-tuple-element.27.refs_8_), channel_id=1, source_target_pairs={{0,3},{1,0},{2,1},{3,2},{4,7},{5,4},{6,5},{7,6},{8,11},{9,8},{10,9... | collective-permute-start | bytes 688136 | tf_op jit(solution)/shard_map/ppermute | solution.py:322
  385.7 68.8 %collective-permute-start.2 = (bf16[2,256,896]{2,1,0:T(8,128)(2,1)}, bf16[2,256,896]{2,1,0:T(8,128)(2,1)}, u32[]{:S(2)}, u32[]{:S(2)}) collective-permute-start(bf16[2,256,896]{2,1,0:T(8,128)(2,1)} %get-tuple-element.24.refs_0_), channel_id=1, source_target_pairs={{0,3},{1,0},{2,1},{3,2},{4,7},{5,4},{6,5},{7,6},{8,11},{9,8},{10,9... | collective-permute-start | bytes 2752520 | tf_op jit(solution)/shard_map/ppermute | solution.py:324
  404.6 49.9 %copy-start.4 = (bf16[2,64,896]{2,1,0:T(8,128)(2,1)}, bf16[2,64,896]{2,1,0:T(8,128)(2,1)S(1)}, u32[]{:S(2)}) copy-start(bf16[2,64,896]{2,1,0:T(8,128)(2,1)S(1)} %collective-permute-done.4.refs_7_) | copy-start | bytes 688132
  404.6 50.1 %collective-permute-start.3 = (bf16[2,256,896]{2,1,0:T(8,128)(2,1)}, bf16[2,256,896]{2,1,0:T(8,128)(2,1)}, u32[]{:S(2)}, u32[]{:S(2)}) collective-permute-start(bf16[2,256,896]{2,1,0:T(8,128)(2,1)} %get-tuple-element.25.refs_2_), channel_id=1, source_target_pairs={{0,1},{1,2},{2,3},{3,0},{4,5},{5,6},{6,7},{7,4},{8,9},{9,10},{10,1... | collective-permute-start | bytes 2752520 | tf_op jit(solution)/shard_map/ppermute | solution.py:324
  409.7 5.6 %copy-start.5 = (bf16[2,64,896]{2,1,0:T(8,128)(2,1)}, bf16[2,64,896]{2,1,0:T(8,128)(2,1)S(1)}, u32[]{:S(2)}) copy-start(bf16[2,64,896]{2,1,0:T(8,128)(2,1)S(1)} %collective-permute-done.5.refs_9_) | copy-start | bytes 688132
  409.7 23.4 %collective-permute-start.6 = (bf16[2,64,896]{2,1,0:T(8,128)(2,1)}, bf16[2,64,896]{2,1,0:T(8,128)(2,1)}, u32[]{:S(2)}, u32[]{:S(2)}) collective-permute-start(bf16[2,64,896]{2,1,0:T(8,128)(2,1)} %get-tuple-element.26.refs_6_), channel_id=1, source_target_pairs={{0,3},{1,0},{2,1},{3,2},{4,7},{5,4},{6,5},{7,6},{8,11},{9,8},{10,9... | collective-permute-start | bytes 688136 | tf_op jit(solution)/shard_map/ppermute | solution.py:324
  412.0 48.1 %collective-permute-start.8 = (bf16[2,256,896]{2,1,0:T(8,128)(2,1)}, bf16[2,256,896]{2,1,0:T(8,128)(2,1)S(1)}, u32[]{:S(2)}, u32[]{:S(2)}) collective-permute-start(bf16[2,256,896]{2,1,0:T(8,128)(2,1)} %collective-permute-done.refs_1_), channel_id=1, source_target_pairs={{0,1},{1,2},{2,3},{3,0},{4,5},{5,6},{6,7},{7,4},{8,9},{9,10},{10,1... | collective-permute-start | bytes 2752520 | tf_op jit(solution)/shard_map/ppermute | solution.py:327
  412.0 19.2 %copy-start.3 = (bf16[2,256,896]{2,1,0:T(8,128)(2,1)}, bf16[2,256,896]{2,1,0:T(8,128)(2,1)S(1)}, u32[]{:S(2)}) copy-start(bf16[2,256,896]{2,1,0:T(8,128)(2,1)S(1)} %collective-permute-done.1.refs_3_) | copy-start | bytes 2752516
  412.1 49.1 %collective-permute-start.9 = (bf16[2,256,896]{2,1,0:T(8,128)(2,1)S(1)}, bf16[2,256,896]{2,1,0:T(8,128)(2,1)S(1)}, u32[]{:S(2)}, u32[]{:S(2)}) collective-permute-start(bf16[2,256,896]{2,1,0:T(8,128)(2,1)S(1)} %collective-permute-done.1.refs_3_), channel_id=1, source_target_pairs={{0,3},{1,0},{2,1},{3,2},{4,7},{5,4},{6,5},{7,6},{8,11},{9,8},{10,9... | collective-permute-start | bytes 2752520 | tf_op jit(solution)/shard_map/ppermute | solution.py:327
  415.3 19.2 %copy-start = (f32[2,640,896]{2,1,0:T(8,128)S(1)}, f32[2,640,896]{2,1,0:T(8,128)}, u32[]{:S(2)}) copy-start(f32[2,640,896]{2,1,0:T(8,128)} %refs_8_.1) | copy-start | bytes 13762564
  415.3 19.2 %copy-start.1 = (f32[2,640,896]{2,1,0:T(8,128)S(1)}, f32[2,640,896]{2,1,0:T(8,128)}, u32[]{:S(2)}) copy-start(f32[2,640,896]{2,1,0:T(8,128)} %refs_11_.1) | copy-start | bytes 13762564
  415.3 19.2 %copy-start.2 = (bf16[2,640,896]{2,1,0:T(8,128)(2,1)S(1)}, bf16[2,640,896]{2,1,0:T(8,128)(2,1)}, u32[]{:S(2)}) copy-start(bf16[2,640,896]{2,1,0:T(8,128)(2,1)} %get-tuple-element.30) | copy-start | bytes 6881284
  433.1 19.4 %collective-permute-start.7 = (bf16[2,64,896]{2,1,0:T(8,128)(2,1)}, bf16[2,64,896]{2,1,0:T(8,128)(2,1)}, u32[]{:S(2)}, u32[]{:S(2)}) collective-permute-start(bf16[2,64,896]{2,1,0:T(8,128)(2,1)} %get-tuple-element.27.refs_8_), channel_id=1, source_target_pairs={{0,1},{1,2},{2,3},{3,0},{4,5},{5,6},{6,7},{7,4},{8,9},{9,10},{10,1... | collective-permute-start | bytes 688136 | tf_op jit(solution)/shard_map/ppermute | solution.py:324
  439.4 13.1 %copy-start.6 = (bf16[2,64,896]{2,1,0:T(8,128)(2,1)S(1)}, bf16[2,64,896]{2,1,0:T(8,128)(2,1)}, u32[]{:S(2)}) copy-start(bf16[2,64,896]{2,1,0:T(8,128)(2,1)} %copy-done.5) | copy-start | bytes 688132
  452.5 9.6 %collective-permute-start.11 = (bf16[2,64,896]{2,1,0:T(8,128)(2,1)S(1)}, bf16[2,64,896]{2,1,0:T(8,128)(2,1)}, u32[]{:S(2)}, u32[]{:S(2)}) collective-permute-start(bf16[2,64,896]{2,1,0:T(8,128)(2,1)S(1)} %copy-done.6), channel_id=1, source_target_pairs={{0,3},{1,0},{2,1},{3,2},{4,7},{5,4},{6,5},{7,6},{8,11},{9,8},{10,9... | collective-permute-start | bytes 688136 | tf_op jit(solution)/shard_map/ppermute | solution.py:327
  454.5 7.6 %collective-permute-start.10 = (bf16[2,64,896]{2,1,0:T(8,128)(2,1)S(1)}, bf16[2,64,896]{2,1,0:T(8,128)(2,1)}, u32[]{:S(2)}, u32[]{:S(2)}) collective-permute-start(bf16[2,64,896]{2,1,0:T(8,128)(2,1)S(1)} %collective-permute-done.4.refs_7_), channel_id=1, source_target_pairs={{0,1},{1,2},{2,3},{3,0},{4,5},{5,6},{6,7},{7,4},{8,9},{9,10},{10,1... | collective-permute-start | bytes 688136 | tf_op jit(solution)/shard_map/ppermute | solution.py:327
